TPU v7x, 32 devices: a whole 2x2x4 slice. The times are simulated.
32 devices in a mesh: data: 2 (over x), dap2: 4 (over z), dap: 4 (over y, core).
Axes of the slice: x: 2, y: 2, z: 4, core: 2. Of those that a mesh axis runs over, the one named last changes fastest.
Arguments:
- pair_act: bfloat16 [768, 384, 128], P(('data', 'dap'), 'dap2'), parts along dimension 0
- pair_mask: int32 [768, 384], P(('data', 'dap'), 'dap2'), parts along dimension 0
- in_gamma: float32 [4, 2, 128], replicated
- in_beta: float32 [4, 2, 128], replicated
- w_proj: bfloat16 [4, 2, 128, 512], replicated
- w_gate: bfloat16 [4, 2, 128, 128], replicated
- out_gamma: float32 [4, 2, 128], replicated
- out_beta: float32 [4, 2, 128], replicated
- w_out: bfloat16 [4, 2, 128, 128], replicated
Outputs:
- output: bfloat16 [768, 384, 128], P(('data', 'dap'), 'dap2'), parts along dimension 0
There are 2 independent parts. A program takes and returns all parts, laid end to end along the dimension named above; an argument that names none is the same for every part.
All inputs are finite; a program needn't handle non-finite values.
Results may differ from a plain program's by a relative error of at most 0.0146083.
Values are sent between devices in bfloat16 or wider.
A program may use at most 1 GiB of HBM per device.

v0:
```python
import jax
import jax.numpy as jnp
from jax import lax
from jax.sharding import PartitionSpec as P

NORM_EPS = 1e-5
OUT_FORM = 'cik,cjk->cij'
IN_FORM = 'cki,ckj->cij'


def layer_norm(values, gamma, beta, axis):
    centered = values - jnp.mean(values, axis=axis, keepdims=True)
    variance = jnp.mean(centered * centered, axis=axis, keepdims=True)
    return centered * lax.rsqrt(variance + NORM_EPS) * gamma + beta


def project_local(pair_blk, mask_f, gamma_in, beta_in, w_proj, w_gate):
    tri_dim = w_proj.shape[1] // 4
    normed = layer_norm(pair_blk.astype(jnp.float32), gamma_in, beta_in, -1).astype(jnp.bfloat16)
    projected = jnp.einsum('ijd,dgc->gcij', normed, w_proj.reshape(w_proj.shape[0], 4, tri_dim), preferred_element_type=jnp.float32)
    left = (mask_f * jax.nn.sigmoid(projected[1]) * projected[0]).astype(jnp.bfloat16)
    right = (mask_f * jax.nn.sigmoid(projected[3]) * projected[2]).astype(jnp.bfloat16)
    gate = jax.nn.sigmoid(jnp.einsum('ijd,de->ije', normed, w_gate, preferred_element_type=jnp.float32))
    return left, right, gate


def finish_local(pair_blk, tri_blk, gate, gamma_out, beta_out, w_out):
    tri_normed = layer_norm(tri_blk.astype(jnp.float32), gamma_out[:, None, None], beta_out[:, None, None], 0).astype(jnp.bfloat16)
    update = jnp.einsum('cij,cd->ijd', tri_normed, w_out, preferred_element_type=jnp.float32)
    return (pair_blk.astype(jnp.float32) + gate * update).astype(jnp.bfloat16)


def to_channels(block):
    col_full = lax.all_to_all(block, 'dap2', 0, 2, tiled=True)
    return lax.all_to_all(col_full, 'dap', 0, 1, tiled=True)


def from_channels(block):
    row_part = lax.all_to_all(block, 'dap', 1, 0, tiled=True)
    return lax.all_to_all(row_part, 'dap2', 2, 0, tiled=True)


def triangle_update(pair_blk, mask_f, params, einsum_form):
    gamma_in, beta_in, w_proj, w_gate, gamma_out, beta_out, w_out = params
    left, right, gate = project_local(pair_blk, mask_f, gamma_in, beta_in, w_proj, w_gate)
    left_ch = to_channels(left)
    right_ch = to_channels(right)
    tri_ch = jnp.einsum(einsum_form, left_ch, right_ch, preferred_element_type=jnp.float32).astype(jnp.bfloat16)
    return finish_local(pair_blk, from_channels(tri_ch), gate, gamma_out, beta_out, w_out)


def solution(mesh):
    pair_spec = P(('data', 'dap'), 'dap2', None)
    mask_spec = P(('data', 'dap'), 'dap2')
    weight_spec = P()

    def local_fn(pair_act, pair_mask, in_gamma, in_beta, w_proj, w_gate, out_gamma, out_beta, w_out):
        mask_f = pair_mask.astype(jnp.float32)
        weights = (in_gamma, in_beta, w_proj, w_gate, out_gamma, out_beta, w_out)
        for layer in range(in_gamma.shape[0]):
            for direction, einsum_form in enumerate((OUT_FORM, IN_FORM)):
                params = tuple(leaf[layer, direction] for leaf in weights)
                pair_act = triangle_update(pair_act, mask_f, params, einsum_form)
        return pair_act

    return jax.shard_map(local_fn, mesh=mesh, in_specs=(pair_spec, mask_spec) + (weight_spec,) * 7, out_specs=pair_spec, check_vma=False)
```

profile of v0, /device:TPU:10, one launch (start us, length us, event | category | flops | bytes accessed | tf_op | source)
XLA Modules:
  0.0 2995.6 jit_solution(8870169965373586550)
XLA Ops:
  30.6 62.4 %all-to-all-done = bf16[128,96,96]{2,1,0:T(8,128)(2,1)} async-done(((bf16[128,96,96]{2,1,0:T(8,128)(2,1)}), bf16[128,96,96]{2,1,0:T(8,128)(2,1)}, u32[]{:S(2)}, u32[]{:S(2)}) %all-to-all-start) | async-done | bytes 2359328 | tf_op jit(solution)/shard_map/all_to_all | solution.py:34
  112.8 54.8 %all-to-all-done.2 = bf16[128,96,96]{2,1,0:T(8,128)(2,1)} async-done(((bf16[128,96,96]{2,1,0:T(8,128)(2,1)}), bf16[128,96,96]{2,1,0:T(8,128)(2,1)}, u32[]{:S(2)}, u32[]{:S(2)}) %all-to-all-start.2) | async-done | bytes 2359328 | tf_op jit(solution)/shard_map/all_to_all | solution.py:34
  238.7 31.0 %all_to_all.792 = bf16[8,384,384]{2,0,1:T(8,128)(2,1)S(1)} all-to-all(bf16[8,384,384]{2,0,1:T(8,128)(2,1)S(1)} %copy.433), channel_id=1, replica_groups=mesh['data'=2,'dap2'=4,'dap'=4] {'dap'}, dimensions={1} | all-to-all | bytes 4718592 | tf_op jit(solution)/shard_map/all_to_all | solution.py:39
  285.5 65.9 %all-to-all-done.5 = bf16[32,96,384]{1,0,2:T(8,128)(2,1)} async-done(((bf16[32,96,384]{1,0,2:T(8,128)(2,1)}), bf16[32,96,384]{1,0,2:T(8,128)(2,1)}, u32[]{:S(2)}, u32[]{:S(2)}) %all-to-all-start.5) | async-done | bytes 2359328 | tf_op jit(solution)/shard_map/all_to_all | solution.py:40
  409.0 62.0 %all-to-all-done.6 = bf16[128,96,96]{2,1,0:T(8,128)(2,1)S(1)} async-done(((bf16[128,96,96]{2,1,0:T(8,128)(2,1)}), bf16[128,96,96]{2,1,0:T(8,128)(2,1)S(1)}, u32[]{:S(2)}, u32[]{:S(2)}) %all-to-all-start.6) | async-done | bytes 2359328 | tf_op jit(solution)/shard_map/all_to_all | solution.py:34
  491.6 54.7 %all-to-all-done.8 = bf16[128,96,96]{2,1,0:T(8,128)(2,1)S(1)} async-done(((bf16[128,96,96]{2,1,0:T(8,128)(2,1)}), bf16[128,96,96]{2,1,0:T(8,128)(2,1)S(1)}, u32[]{:S(2)}, u32[]{:S(2)}) %all-to-all-start.8) | async-done | bytes 2359328 | tf_op jit(solution)/shard_map/all_to_all | solution.py:34
  617.2 31.0 %all_to_all.793 = bf16[8,384,384]{2,0,1:T(8,128)(2,1)S(1)} all-to-all(bf16[8,384,384]{2,0,1:T(8,128)(2,1)S(1)} %copy.452), channel_id=1, replica_groups=mesh['data'=2,'dap2'=4,'dap'=4] {'dap'}, dimensions={1} | all-to-all | bytes 4718592 | tf_op jit(solution)/shard_map/all_to_all | solution.py:39
  660.6 65.4 %all-to-all-done.11 = bf16[32,96,384]{1,0,2:T(8,128)(2,1)S(1)} async-done(((bf16[32,96,384]{1,0,2:T(8,128)(2,1)}), bf16[32,96,384]{1,0,2:T(8,128)(2,1)S(1)}, u32[]{:S(2)}, u32[]{:S(2)}) %all-to-all-start.11) | async-done | bytes 2359328 | tf_op jit(solution)/shard_map/all_to_all | solution.py:40
  782.0 61.9 %all-to-all-done.12 = bf16[128,96,96]{2,1,0:T(8,128)(2,1)S(1)} async-done(((bf16[128,96,96]{2,1,0:T(8,128)(2,1)}), bf16[128,96,96]{2,1,0:T(8,128)(2,1)S(1)}, u32[]{:S(2)}, u32[]{:S(2)}) %all-to-all-start.12) | async-done | bytes 2359328 | tf_op jit(solution)/shard_map/all_to_all | solution.py:34
  864.5 54.7 %all-to-all-done.14 = bf16[128,96,96]{2,1,0:T(8,128)(2,1)S(1)} async-done(((bf16[128,96,96]{2,1,0:T(8,128)(2,1)}), bf16[128,96,96]{2,1,0:T(8,128)(2,1)S(1)}, u32[]{:S(2)}, u32[]{:S(2)}) %all-to-all-start.14) | async-done | bytes 2359328 | tf_op jit(solution)/shard_map/all_to_all | solution.py:34
  990.1 31.0 %all_to_all.794 = bf16[8,384,384]{2,0,1:T(8,128)(2,1)S(1)} all-to-all(bf16[8,384,384]{2,0,1:T(8,128)(2,1)S(1)} %copy.470), channel_id=1, replica_groups=mesh['data'=2,'dap2'=4,'dap'=4] {'dap'}, dimensions={1} | all-to-all | bytes 4718592 | tf_op jit(solution)/shard_map/all_to_all | solution.py:39
  1033.5 65.4 %all-to-all-done.17 = bf16[32,96,384]{1,0,2:T(8,128)(2,1)S(1)} async-done(((bf16[32,96,384]{1,0,2:T(8,128)(2,1)}), bf16[32,96,384]{1,0,2:T(8,128)(2,1)S(1)}, u32[]{:S(2)}, u32[]{:S(2)}) %all-to-all-start.17) | async-done | bytes 2359328 | tf_op jit(solution)/shard_map/all_to_all | solution.py:40
  1154.9 61.9 %all-to-all-done.18 = bf16[128,96,96]{2,1,0:T(8,128)(2,1)S(1)} async-done(((bf16[128,96,96]{2,1,0:T(8,128)(2,1)}), bf16[128,96,96]{2,1,0:T(8,128)(2,1)S(1)}, u32[]{:S(2)}, u32[]{:S(2)}) %all-to-all-start.18) | async-done | bytes 2359328 | tf_op jit(solution)/shard_map/all_to_all | solution.py:34
  1237.4 54.7 %all-to-all-done.20 = bf16[128,96,96]{2,1,0:T(8,128)(2,1)S(1)} async-done(((bf16[128,96,96]{2,1,0:T(8,128)(2,1)}), bf16[128,96,96]{2,1,0:T(8,128)(2,1)S(1)}, u32[]{:S(2)}, u32[]{:S(2)}) %all-to-all-start.20) | async-done | bytes 2359328 | tf_op jit(solution)/shard_map/all_to_all | solution.py:34
  1363.0 31.0 %all_to_all.795 = bf16[8,384,384]{2,0,1:T(8,128)(2,1)S(1)} all-to-all(bf16[8,384,384]{2,0,1:T(8,128)(2,1)S(1)} %copy.489), channel_id=1, replica_groups=mesh['data'=2,'dap2'=4,'dap'=4] {'dap'}, dimensions={1} | all-to-all | bytes 4718592 | tf_op jit(solution)/shard_map/all_to_all | solution.py:39
  1406.4 65.4 %all-to-all-done.23 = bf16[32,96,384]{1,0,2:T(8,128)(2,1)S(1)} async-done(((bf16[32,96,384]{1,0,2:T(8,128)(2,1)}), bf16[32,96,384]{1,0,2:T(8,128)(2,1)S(1)}, u32[]{:S(2)}, u32[]{:S(2)}) %all-to-all-start.23) | async-done | bytes 2359328 | tf_op jit(solution)/shard_map/all_to_all | solution.py:40
  1527.8 61.9 %all-to-all-done.24 = bf16[128,96,96]{2,1,0:T(8,128)(2,1)S(1)} async-done(((bf16[128,96,96]{2,1,0:T(8,128)(2,1)}), bf16[128,96,96]{2,1,0:T(8,128)(2,1)S(1)}, u32[]{:S(2)}, u32[]{:S(2)}) %all-to-all-start.24) | async-done | bytes 2359328 | tf_op jit(solution)/shard_map/all_to_all | solution.py:34
  1610.3 54.7 %all-to-all-done.26 = bf16[128,96,96]{2,1,0:T(8,128)(2,1)S(1)} async-done(((bf16[128,96,96]{2,1,0:T(8,128)(2,1)}), bf16[128,96,96]{2,1,0:T(8,128)(2,1)S(1)}, u32[]{:S(2)}, u32[]{:S(2)}) %all-to-all-start.26) | async-done | bytes 2359328 | tf_op jit(solution)/shard_map/all_to_all | solution.py:34
  1735.9 31.0 %all_to_all.796 = bf16[8,384,384]{2,0,1:T(8,128)(2,1)S(1)} all-to-all(bf16[8,384,384]{2,0,1:T(8,128)(2,1)S(1)} %copy.507), channel_id=1, replica_groups=mesh['data'=2,'dap2'=4,'dap'=4] {'dap'}, dimensions={1} | all-to-all | bytes 4718592 | tf_op jit(solution)/shard_map/all_to_all | solution.py:39
  1779.3 65.4 %all-to-all-done.29 = bf16[32,96,384]{1,0,2:T(8,128)(2,1)S(1)} async-done(((bf16[32,96,384]{1,0,2:T(8,128)(2,1)}), bf16[32,96,384]{1,0,2:T(8,128)(2,1)S(1)}, u32[]{:S(2)}, u32[]{:S(2)}) %all-to-all-start.29) | async-done | bytes 2359328 | tf_op jit(solution)/shard_map/all_to_all | solution.py:40
  1900.7 61.9 %all-to-all-done.30 = bf16[128,96,96]{2,1,0:T(8,128)(2,1)S(1)} async-done(((bf16[128,96,96]{2,1,0:T(8,128)(2,1)}), bf16[128,96,96]{2,1,0:T(8,128)(2,1)S(1)}, u32[]{:S(2)}, u32[]{:S(2)}) %all-to-all-start.30) | async-done | bytes 2359328 | tf_op jit(solution)/shard_map/all_to_all | solution.py:34
  1983.2 54.7 %all-to-all-done.32 = bf16[128,96,96]{2,1,0:T(8,128)(2,1)S(1)} async-done(((bf16[128,96,96]{2,1,0:T(8,128)(2,1)}), bf16[128,96,96]{2,1,0:T(8,128)(2,1)S(1)}, u32[]{:S(2)}, u32[]{:S(2)}) %all-to-all-start.32) | async-done | bytes 2359328 | tf_op jit(solution)/shard_map/all_to_all | solution.py:34
  2108.8 31.0 %all_to_all.797 = bf16[8,384,384]{2,0,1:T(8,128)(2,1)S(1)} all-to-all(bf16[8,384,384]{2,0,1:T(8,128)(2,1)S(1)} %copy.526), channel_id=1, replica_groups=mesh['data'=2,'dap2'=4,'dap'=4] {'dap'}, dimensions={1} | all-to-all | bytes 4718592 | tf_op jit(solution)/shard_map/all_to_all | solution.py:39
  2152.2 65.4 %all-to-all-done.35 = bf16[32,96,384]{1,0,2:T(8,128)(2,1)S(1)} async-done(((bf16[32,96,384]{1,0,2:T(8,128)(2,1)}), bf16[32,96,384]{1,0,2:T(8,128)(2,1)S(1)}, u32[]{:S(2)}, u32[]{:S(2)}) %all-to-all-start.35) | async-done | bytes 2359328 | tf_op jit(solution)/shard_map/all_to_all | solution.py:40
  2273.6 61.9 %all-to-all-done.36 = bf16[128,96,96]{2,1,0:T(8,128)(2,1)S(1)} async-done(((bf16[128,96,96]{2,1,0:T(8,128)(2,1)}), bf16[128,96,96]{2,1,0:T(8,128)(2,1)S(1)}, u32[]{:S(2)}, u32[]{:S(2)}) %all-to-all-start.36) | async-done | bytes 2359328 | tf_op jit(solution)/shard_map/all_to_all | solution.py:34
  2356.1 54.7 %all-to-all-done.38 = bf16[128,96,96]{2,1,0:T(8,128)(2,1)S(1)} async-done(((bf16[128,96,96]{2,1,0:T(8,128)(2,1)}), bf16[128,96,96]{2,1,0:T(8,128)(2,1)S(1)}, u32[]{:S(2)}, u32[]{:S(2)}) %all-to-all-start.38) | async-done | bytes 2359328 | tf_op jit(solution)/shard_map/all_to_all | solution.py:34
  2481.8 31.0 %all_to_all.798 = bf16[8,384,384]{2,0,1:T(8,128)(2,1)S(1)} all-to-all(bf16[8,384,384]{2,0,1:T(8,128)(2,1)S(1)} %copy.544), channel_id=1, replica_groups=mesh['data'=2,'dap2'=4,'dap'=4] {'dap'}, dimensions={1} | all-to-all | bytes 4718592 | tf_op jit(solution)/shard_map/all_to_all | solution.py:39
  2525.1 65.4 %all-to-all-done.41 = bf16[32,96,384]{1,0,2:T(8,128)(2,1)S(1)} async-done(((bf16[32,96,384]{1,0,2:T(8,128)(2,1)}), bf16[32,96,384]{1,0,2:T(8,128)(2,1)S(1)}, u32[]{:S(2)}, u32[]{:S(2)}) %all-to-all-start.41) | async-done | bytes 2359328 | tf_op jit(solution)/shard_map/all_to_all | solution.py:40
  2646.6 61.9 %all-to-all-done.42 = bf16[128,96,96]{2,1,0:T(8,128)(2,1)S(1)} async-done(((bf16[128,96,96]{2,1,0:T(8,128)(2,1)}), bf16[128,96,96]{2,1,0:T(8,128)(2,1)S(1)}, u32[]{:S(2)}, u32[]{:S(2)}) %all-to-all-start.42) | async-done | bytes 2359328 | tf_op jit(solution)/shard_map/all_to_all | solution.py:34
  2729.2 54.7 %all-to-all-done.44 = bf16[128,96,96]{2,1,0:T(8,128)(2,1)S(1)} async-done(((bf16[128,96,96]{2,1,0:T(8,128)(2,1)}), bf16[128,96,96]{2,1,0:T(8,128)(2,1)S(1)}, u32[]{:S(2)}, u32[]{:S(2)}) %all-to-all-start.44) | async-done | bytes 2359328 | tf_op jit(solution)/shard_map/all_to_all | solution.py:34
  2854.6 31.0 %all_to_all.799 = bf16[8,384,384]{2,0,1:T(8,128)(2,1)S(1)} all-to-all(bf16[8,384,384]{2,0,1:T(8,128)(2,1)S(1)} %copy.563), channel_id=1, replica_groups=mesh['data'=2,'dap2'=4,'dap'=4] {'dap'}, dimensions={1} | all-to-all | bytes 4718592 | tf_op jit(solution)/shard_map/all_to_all | solution.py:39
  2896.6 66.7 %all-to-all-done.47 = bf16[32,96,384]{1,0,2:T(8,128)(2,1)S(1)} async-done(((bf16[32,96,384]{1,0,2:T(8,128)(2,1)}), bf16[32,96,384]{1,0,2:T(8,128)(2,1)S(1)}, u32[]{:S(2)}, u32[]{:S(2)}) %all-to-all-start.47) | async-done | bytes 2359328 | tf_op jit(solution)/shard_map/all_to_all | solution.py:40
  (503 shorter events, 1286.7 us)
Async XLA Ops:
  20.5 72.5 %all-to-all-start = ((bf16[128,96,96]{2,1,0:T(8,128)(2,1)}), bf16[128,96,96]{2,1,0:T(8,128)(2,1)}, u32[]{:S(2)}, u32[]{:S(2)}) async-start(bf16[128,96,96]{2,1,0:T(8,128)(2,1)} %copy.426), calls=%async_computation | async-start | bytes 6291456 | tf_op jit(solution)/shard_map/all_to_all | solution.py:34
  92.9 74.7 %all-to-all-start.2 = ((bf16[128,96,96]{2,1,0:T(8,128)(2,1)}), bf16[128,96,96]{2,1,0:T(8,128)(2,1)}, u32[]{:S(2)}, u32[]{:S(2)}) async-start(bf16[128,96,96]{2,1,0:T(8,128)(2,1)} %copy.430), calls=%async_computation.2 | async-start | bytes 6291456 | tf_op jit(solution)/shard_map/all_to_all | solution.py:34
  167.6 32.9 %all-to-all-start.1 = ((bf16[32,96,384]{2,1,0:T(8,128)(2,1)}), bf16[32,96,384]{2,1,0:T(8,128)(2,1)}, u32[]{:S(2)}, u32[]{:S(2)}) async-start(bf16[32,96,384]{2,1,0:T(8,128)(2,1)} %all_to_all.579), calls=%async_computation.1 | async-start | bytes 4718592 | tf_op jit(solution)/shard_map/all_to_all | solution.py:35
  276.5 74.9 %all-to-all-start.5 = ((bf16[32,96,384]{1,0,2:T(8,128)(2,1)}), bf16[32,96,384]{1,0,2:T(8,128)(2,1)}, u32[]{:S(2)}, u32[]{:S(2)}) async-start(bf16[32,96,384]{1,0,2:T(8,128)(2,1)} %copy.436), calls=%async_computation.5 | async-start | bytes 6291456 | tf_op jit(solution)/shard_map/all_to_all | solution.py:40
  397.3 73.7 %all-to-all-start.6 = ((bf16[128,96,96]{2,1,0:T(8,128)(2,1)}), bf16[128,96,96]{2,1,0:T(8,128)(2,1)S(1)}, u32[]{:S(2)}, u32[]{:S(2)}) async-start(bf16[128,96,96]{2,1,0:T(8,128)(2,1)} %copy.445), calls=%async_computation.6 | async-start | bytes 6291456 | tf_op jit(solution)/shard_map/all_to_all | solution.py:34
  472.7 73.6 %all-to-all-start.8 = ((bf16[128,96,96]{2,1,0:T(8,128)(2,1)}), bf16[128,96,96]{2,1,0:T(8,128)(2,1)S(1)}, u32[]{:S(2)}, u32[]{:S(2)}) async-start(bf16[128,96,96]{2,1,0:T(8,128)(2,1)} %copy.448), calls=%async_computation.8 | async-start | bytes 6291456 | tf_op jit(solution)/shard_map/all_to_all | solution.py:34
  579.1 33.1 %all-to-all-start.9 = ((bf16[32,96,384]{2,1,0:T(8,128)(2,1)}), bf16[32,96,384]{2,1,0:T(8,128)(2,1)}, u32[]{:S(2)}, u32[]{:S(2)}) async-start(bf16[32,96,384]{2,1,0:T(8,128)(2,1)} %all_to_all.608), calls=%async_computation.9 | async-start | bytes 4718592 | tf_op jit(solution)/shard_map/all_to_all | solution.py:35
  652.0 74.0 %all-to-all-start.11 = ((bf16[32,96,384]{1,0,2:T(8,128)(2,1)}), bf16[32,96,384]{1,0,2:T(8,128)(2,1)S(1)}, u32[]{:S(2)}, u32[]{:S(2)}) async-start(bf16[32,96,384]{1,0,2:T(8,128)(2,1)} %copy.455), calls=%async_computation.11 | async-start | bytes 6291456 | tf_op jit(solution)/shard_map/all_to_all | solution.py:40
  770.3 73.6 %all-to-all-start.12 = ((bf16[128,96,96]{2,1,0:T(8,128)(2,1)}), bf16[128,96,96]{2,1,0:T(8,128)(2,1)S(1)}, u32[]{:S(2)}, u32[]{:S(2)}) async-start(bf16[128,96,96]{2,1,0:T(8,128)(2,1)} %copy.464), calls=%async_computation.12 | async-start | bytes 6291456 | tf_op jit(solution)/shard_map/all_to_all | solution.py:34
  845.6 73.6 %all-to-all-start.14 = ((bf16[128,96,96]{2,1,0:T(8,128)(2,1)}), bf16[128,96,96]{2,1,0:T(8,128)(2,1)S(1)}, u32[]{:S(2)}, u32[]{:S(2)}) async-start(bf16[128,96,96]{2,1,0:T(8,128)(2,1)} %copy.467), calls=%async_computation.14 | async-start | bytes 6291456 | tf_op jit(solution)/shard_map/all_to_all | solution.py:34
  951.9 33.1 %all-to-all-start.15 = ((bf16[32,96,384]{2,1,0:T(8,128)(2,1)}), bf16[32,96,384]{2,1,0:T(8,128)(2,1)}, u32[]{:S(2)}, u32[]{:S(2)}) async-start(bf16[32,96,384]{2,1,0:T(8,128)(2,1)} %all_to_all.629), calls=%async_computation.15 | async-start | bytes 4718592 | tf_op jit(solution)/shard_map/all_to_all | solution.py:35
  1024.9 74.0 %all-to-all-start.17 = ((bf16[32,96,384]{1,0,2:T(8,128)(2,1)}), bf16[32,96,384]{1,0,2:T(8,128)(2,1)S(1)}, u32[]{:S(2)}, u32[]{:S(2)}) async-start(bf16[32,96,384]{1,0,2:T(8,128)(2,1)} %copy.473), calls=%async_computation.17 | async-start | bytes 6291456 | tf_op jit(solution)/shard_map/all_to_all | solution.py:40
  1143.2 73.6 %all-to-all-start.18 = ((bf16[128,96,96]{2,1,0:T(8,128)(2,1)}), bf16[128,96,96]{2,1,0:T(8,128)(2,1)S(1)}, u32[]{:S(2)}, u32[]{:S(2)}) async-start(bf16[128,96,96]{2,1,0:T(8,128)(2,1)} %copy.482), calls=%async_computation.18 | async-start | bytes 6291456 | tf_op jit(solution)/shard_map/all_to_all | solution.py:34
  1218.5 73.6 %all-to-all-start.20 = ((bf16[128,96,96]{2,1,0:T(8,128)(2,1)}), bf16[128,96,96]{2,1,0:T(8,128)(2,1)S(1)}, u32[]{:S(2)}, u32[]{:S(2)}) async-start(bf16[128,96,96]{2,1,0:T(8,128)(2,1)} %copy.485), calls=%async_computation.20 | async-start | bytes 6291456 | tf_op jit(solution)/shard_map/all_to_all | solution.py:34
  1324.8 33.1 %all-to-all-start.21 = ((bf16[32,96,384]{2,1,0:T(8,128)(2,1)}), bf16[32,96,384]{2,1,0:T(8,128)(2,1)}, u32[]{:S(2)}, u32[]{:S(2)}) async-start(bf16[32,96,384]{2,1,0:T(8,128)(2,1)} %all_to_all.650), calls=%async_computation.21 | async-start | bytes 4718592 | tf_op jit(solution)/shard_map/all_to_all | solution.py:35
  1397.8 74.0 %all-to-all-start.23 = ((bf16[32,96,384]{1,0,2:T(8,128)(2,1)}), bf16[32,96,384]{1,0,2:T(8,128)(2,1)S(1)}, u32[]{:S(2)}, u32[]{:S(2)}) async-start(bf16[32,96,384]{1,0,2:T(8,128)(2,1)} %copy.492), calls=%async_computation.23 | async-start | bytes 6291456 | tf_op jit(solution)/shard_map/all_to_all | solution.py:40
  1516.1 73.6 %all-to-all-start.24 = ((bf16[128,96,96]{2,1,0:T(8,128)(2,1)}), bf16[128,96,96]{2,1,0:T(8,128)(2,1)S(1)}, u32[]{:S(2)}, u32[]{:S(2)}) async-start(bf16[128,96,96]{2,1,0:T(8,128)(2,1)} %copy.501), calls=%async_computation.24 | async-start | bytes 6291456 | tf_op jit(solution)/shard_map/all_to_all | solution.py:34
  1591.4 73.6 %all-to-all-start.26 = ((bf16[128,96,96]{2,1,0:T(8,128)(2,1)}), bf16[128,96,96]{2,1,0:T(8,128)(2,1)S(1)}, u32[]{:S(2)}, u32[]{:S(2)}) async-start(bf16[128,96,96]{2,1,0:T(8,128)(2,1)} %copy.504), calls=%async_computation.26 | async-start | bytes 6291456 | tf_op jit(solution)/shard_map/all_to_all | solution.py:34
  1697.7 33.1 %all-to-all-start.27 = ((bf16[32,96,384]{2,1,0:T(8,128)(2,1)}), bf16[32,96,384]{2,1,0:T(8,128)(2,1)}, u32[]{:S(2)}, u32[]{:S(2)}) async-start(bf16[32,96,384]{2,1,0:T(8,128)(2,1)} %all_to_all.671), calls=%async_computation.27 | async-start | bytes 4718592 | tf_op jit(solution)/shard_map/all_to_all | solution.py:35
  1770.7 74.0 %all-to-all-start.29 = ((bf16[32,96,384]{1,0,2:T(8,128)(2,1)}), bf16[32,96,384]{1,0,2:T(8,128)(2,1)S(1)}, u32[]{:S(2)}, u32[]{:S(2)}) async-start(bf16[32,96,384]{1,0,2:T(8,128)(2,1)} %copy.510), calls=%async_computation.29 | async-start | bytes 6291456 | tf_op jit(solution)/shard_map/all_to_all | solution.py:40
  1889.0 73.6 %all-to-all-start.30 = ((bf16[128,96,96]{2,1,0:T(8,128)(2,1)}), bf16[128,96,96]{2,1,0:T(8,128)(2,1)S(1)}, u32[]{:S(2)}, u32[]{:S(2)}) async-start(bf16[128,96,96]{2,1,0:T(8,128)(2,1)} %copy.519), calls=%async_computation.30 | async-start | bytes 6291456 | tf_op jit(solution)/shard_map/all_to_all | solution.py:34
  1964.3 73.6 %all-to-all-start.32 = ((bf16[128,96,96]{2,1,0:T(8,128)(2,1)}), bf16[128,96,96]{2,1,0:T(8,128)(2,1)S(1)}, u32[]{:S(2)}, u32[]{:S(2)}) async-start(bf16[128,96,96]{2,1,0:T(8,128)(2,1)} %copy.522), calls=%async_computation.32 | async-start | bytes 6291456 | tf_op jit(solution)/shard_map/all_to_all | solution.py:34
  2070.7 33.1 %all-to-all-start.33 = ((bf16[32,96,384]{2,1,0:T(8,128)(2,1)}), bf16[32,96,384]{2,1,0:T(8,128)(2,1)}, u32[]{:S(2)}, u32[]{:S(2)}) async-start(bf16[32,96,384]{2,1,0:T(8,128)(2,1)} %all_to_all.692), calls=%async_computation.33 | async-start | bytes 4718592 | tf_op jit(solution)/shard_map/all_to_all | solution.py:35
  2143.6 74.0 %all-to-all-start.35 = ((bf16[32,96,384]{1,0,2:T(8,128)(2,1)}), bf16[32,96,384]{1,0,2:T(8,128)(2,1)S(1)}, u32[]{:S(2)}, u32[]{:S(2)}) async-start(bf16[32,96,384]{1,0,2:T(8,128)(2,1)} %copy.529), calls=%async_computation.35 | async-start | bytes 6291456 | tf_op jit(solution)/shard_map/all_to_all | solution.py:40
  2261.9 73.6 %all-to-all-start.36 = ((bf16[128,96,96]{2,1,0:T(8,128)(2,1)}), bf16[128,96,96]{2,1,0:T(8,128)(2,1)S(1)}, u32[]{:S(2)}, u32[]{:S(2)}) async-start(bf16[128,96,96]{2,1,0:T(8,128)(2,1)} %copy.538), calls=%async_computation.36 | async-start | bytes 6291456 | tf_op jit(solution)/shard_map/all_to_all | solution.py:34
  2337.2 73.6 %all-to-all-start.38 = ((bf16[128,96,96]{2,1,0:T(8,128)(2,1)}), bf16[128,96,96]{2,1,0:T(8,128)(2,1)S(1)}, u32[]{:S(2)}, u32[]{:S(2)}) async-start(bf16[128,96,96]{2,1,0:T(8,128)(2,1)} %copy.541), calls=%async_computation.38 | async-start | bytes 6291456 | tf_op jit(solution)/shard_map/all_to_all | solution.py:34
  2443.6 33.1 %all-to-all-start.39 = ((bf16[32,96,384]{2,1,0:T(8,128)(2,1)}), bf16[32,96,384]{2,1,0:T(8,128)(2,1)}, u32[]{:S(2)}, u32[]{:S(2)}) async-start(bf16[32,96,384]{2,1,0:T(8,128)(2,1)} %all_to_all.713), calls=%async_computation.39 | async-start | bytes 4718592 | tf_op jit(solution)/shard_map/all_to_all | solution.py:35
  2516.5 74.0 %all-to-all-start.41 = ((bf16[32,96,384]{1,0,2:T(8,128)(2,1)}), bf16[32,96,384]{1,0,2:T(8,128)(2,1)S(1)}, u32[]{:S(2)}, u32[]{:S(2)}) async-start(bf16[32,96,384]{1,0,2:T(8,128)(2,1)} %copy.547), calls=%async_computation.41 | async-start | bytes 6291456 | tf_op jit(solution)/shard_map/all_to_all | solution.py:40
  2634.9 73.6 %all-to-all-start.42 = ((bf16[128,96,96]{2,1,0:T(8,128)(2,1)}), bf16[128,96,96]{2,1,0:T(8,128)(2,1)S(1)}, u32[]{:S(2)}, u32[]{:S(2)}) async-start(bf16[128,96,96]{2,1,0:T(8,128)(2,1)} %copy.556), calls=%async_computation.42 | async-start | bytes 6291456 | tf_op jit(solution)/shard_map/all_to_all | solution.py:34
  2710.3 73.6 %all-to-all-start.44 = ((bf16[128,96,96]{2,1,0:T(8,128)(2,1)}), bf16[128,96,96]{2,1,0:T(8,128)(2,1)S(1)}, u32[]{:S(2)}, u32[]{:S(2)}) async-start(bf16[128,96,96]{2,1,0:T(8,128)(2,1)} %copy.559), calls=%async_computation.44 | async-start | bytes 6291456 | tf_op jit(solution)/shard_map/all_to_all | solution.py:34
  2816.6 32.9 %all-to-all-start.45 = ((bf16[32,96,384]{2,1,0:T(8,128)(2,1)}), bf16[32,96,384]{2,1,0:T(8,128)(2,1)}, u32[]{:S(2)}, u32[]{:S(2)}) async-start(bf16[32,96,384]{2,1,0:T(8,128)(2,1)} %all_to_all.734), calls=%async_computation.45 | async-start | bytes 4718592 | tf_op jit(solution)/shard_map/all_to_all | solution.py:35
  2889.3 74.0 %all-to-all-start.47 = ((bf16[32,96,384]{1,0,2:T(8,128)(2,1)}), bf16[32,96,384]{1,0,2:T(8,128)(2,1)S(1)}, u32[]{:S(2)}, u32[]{:S(2)}) async-start(bf16[32,96,384]{1,0,2:T(8,128)(2,1)} %copy.566), calls=%async_computation.47 | async-start | bytes 6291456 | tf_op jit(solution)/shard_map/all_to_all | solution.py:40
  (101 other events, 1553.1 us)
where the time goes:
time: 3020 us; the launch traced here: 3000 us
  waiting for transfers between devices  1810 us (60%)
  local copies, waits for them, and re-layouts  464 us (15%)
  blocking collectives  248 us (8%)
  starting transfers between devices  241 us (8%)
  other arithmetic  132 us (4%)
  matrix products  96.7 us (3%)
    all_to_all x16, waiting for transfers between devices, to_channels(): col_full = lax.all_to_all(block, 'dap2', 0, 2, tiled=True)  934 us
    all_to_all x8, waiting for transfers between devices, from_channels(): return lax.all_to_all(row_part, 'dap2', 2, 0, tiled=True)  525 us
    all_to_all x16, waiting for transfers between devices, to_channels(): return lax.all_to_all(col_full, 'dap', 0, 1, tiled=True)  352 us
    all_to_all x8, blocking collectives, from_channels(): row_part = lax.all_to_all(block, 'dap', 1, 0, tiled=True)  248 us
    all_to_all x32, local copies, waits for them, and re-layouts, to_channels(): col_full = lax.all_to_all(block, 'dap2', 0, 2, tiled=True)  178 us
    all_to_all x16, starting transfers between devices, to_channels(): col_full = lax.all_to_all(block, 'dap2', 0, 2, tiled=True)  110 us
    all_to_all x16, starting transfers between devices, to_channels(): return lax.all_to_all(col_full, 'dap', 0, 1, tiled=True)  74.7 us
  transfers between devices with their start and end apart: 40, of which 40 were waited for; matrix products, arithmetic and copies ran while one was open for 5% of the time, Pallas kernels for 0%

commit v1 on v0

v1 whole, which is shorter than its diff:
```python
import functools

import jax
import jax.numpy as jnp
from jax import lax
from jax.experimental import pallas as pl
from jax.experimental.pallas import tpu as pltpu
from jax.sharding import PartitionSpec as P

NORM_EPS = 1e-5
MESH = pl.DeviceIdType.MESH
N = 384
C = 128
D = 16
ROWS = N // D
BLK = 96
CPD = C // D
CHUNK = 8
NCHUNK = ROWS // CHUNK
LT = N // 128
UPDATES = 8


def sigmoid(x):
    return 0.5 * jnp.tanh(0.5 * x) + 0.5


def norm_channels(v, gamma, beta):
    mean = jnp.sum(v, axis=0, keepdims=True) * (1.0 / C)
    centered = v - mean
    variance = jnp.sum(centered * centered, axis=0, keepdims=True) * (1.0 / C)
    return centered * lax.rsqrt(variance + NORM_EPS) * gamma + beta


def kernel(z_in, m_in, gin, bin_, wp, wg, gout, bout, wo, out,
           zrow, mrow, mask, z, gate, x, q, y, ab, r, s, t, tsend, trecv,
           zsend_sem, msend_sem, zrecv_sem, mrecv_sem, absend_sem, abrecv_sem, tsend_sem, trecv_sem,
           osend_sem, orecv_sem):
    g = lax.axis_index("data")
    jz = lax.axis_index("dap2")
    iy = lax.axis_index("dap")
    half = jz // 2
    zl = jz % 2
    me = g * 8 + zl * 4 + iy
    row0 = me * ROWS

    def place(d):
        px = (g + d // 8) % 2
        pz = (zl + (d // 4) % 2) % 2
        py = (iy + d % 4) % 4
        return (px, 2 * half + pz, py), px * 8 + pz * 4 + py

    def blocks_out(q_, start):
        here = jnp.logical_and(jnp.logical_and(iy // 2 == g, jz == 2 * g + iy % 2), iy == q_)
        dst = (iy // 2, 2 * g + iy % 2, q_)
        rows = pl.ds(q_ * ROWS, ROWS)
        cols = pl.ds(pl.multiple_of(jz * BLK, 32), BLK)
        for src, dst_ref, send, recv in (
            (z_in.at[rows], zrow.at[:, cols, :], zsend_sem.at[q_], zrecv_sem),
            (m_in.at[rows], mrow.at[jz], msend_sem.at[q_], mrecv_sem),
        ):
            @pl.when(jnp.logical_not(here))
            def _():
                copy = pltpu.make_async_remote_copy(src, dst_ref, send, recv, device_id=dst, device_id_type=MESH)
                if start:
                    copy.start()
                else:
                    copy.wait_send()

            if start:
                @pl.when(here)
                def _():
                    pltpu.make_async_copy(src, dst_ref, recv).start()

    for q_ in range(4):
        blocks_out(q_, True)
    pltpu.make_async_copy(mrow, mrow, mrecv_sem).wait()
    pltpu.make_async_copy(zrow, zrow, zrecv_sem).wait()
    lane = lax.broadcasted_iota(jnp.int32, (128, N), 0)
    col = lax.broadcasted_iota(jnp.int32, (128, N), 1)
    total = jnp.zeros((ROWS, N), jnp.float32)
    for j in range(4):
        pick = jnp.logical_and(col == lane + j * BLK, lane < BLK).astype(jnp.float32)
        total = total + jnp.dot(mrow[j], pick, preferred_element_type=jnp.float32)
    mask[...] = total
    for q_ in range(4):
        blocks_out(q_, False)

    def turn_in(i, _):
        z[i] = zrow[i].T
        return 0

    lax.fori_loop(0, ROWS, turn_in, 0)

    def project(u, p):
        for h in range(2):
            for lt in range(LT):
                v = z[2 * p + h, :, pl.ds(lt * 128, 128)].astype(jnp.float32)
                xn = norm_channels(v, gin[u], bin_[u])
                x[:, pl.ds(h * N + lt * 128, 128)] = xn.astype(jnp.bfloat16)
        q[pl.ds(0, 4 * C), :] = jnp.dot(wp[u], x[...], preferred_element_type=jnp.float32)
        q[pl.ds(4 * C, C), :] = jnp.dot(wg[u], x[...], preferred_element_type=jnp.float32)
        for h in range(2):
            cols = pl.ds(h * N, N)
            m = mask[pl.ds(2 * p + h, 1), :]
            for d in range(D):
                def part(k):
                    return q[pl.ds(k * C + d * CPD, CPD), cols]
                left = m * sigmoid(part(1)) * part(0)
                right = m * sigmoid(part(3)) * part(2)
                ab[d, 2 * p + h] = jnp.concatenate([left, right], axis=0).astype(jnp.bfloat16)
                gate[2 * p + h, pl.ds(d * CPD, CPD), :] = sigmoid(part(4))

    def finish(u, p):
        for lt in range(LT):
            tv = trecv[:, p, :, pl.ds(lt * 128, 128)].astype(jnp.float32)
            for h in range(2):
                v = tv[:, h * CPD:(h + 1) * CPD, :].reshape(C, 128)
                yn = norm_channels(v, gout[u], bout[u])
                y[:, pl.ds(h * N + lt * 128, 128)] = yn.astype(jnp.bfloat16)
        q[pl.ds(0, C), :] = jnp.dot(wo[u], y[...], preferred_element_type=jnp.float32)
        for h in range(2):
            for k in range(C // 16):
                rows = pl.ds(k * 16, 16)
                upd = gate[2 * p + h, rows, :] * q[rows, pl.ds(h * N, N)]
                z[2 * p + h, rows, :] = (z[2 * p + h, rows, :].astype(jnp.float32) + upd).astype(jnp.bfloat16)

    def send_ab(c):
        mine = pl.ds(pl.multiple_of(row0 + c * CHUNK, 8), CHUNK)
        rows = pl.ds(c * CHUNK, CHUNK)

        def to(d, _):
            dst, num = place(d)
            pltpu.make_async_remote_copy(ab.at[num, rows], r.at[mine], absend_sem, abrecv_sem.at[c],
                                         device_id=dst, device_id_type=MESH).start()
            return 0

        lax.fori_loop(1, D, to, 0)
        r[mine] = ab[me, rows]

    def project_chunk(u, c):
        def one(p, _):
            project(u, c * (CHUNK // 2) + p)
            return 0

        lax.fori_loop(0, CHUNK // 2, one, 0)
        send_ab(c)

    for c in range(NCHUNK):
        project_chunk(0, c)

    def update(u, _):
        for c in range(NCHUNK):
            part = r.at[pl.ds(0, (D - 1) * CHUNK)]
            pltpu.make_async_copy(part, part, abrecv_sem.at[c]).wait()

            def turn(k, _):
                rows = pl.ds(pl.multiple_of(k * ROWS + c * CHUNK, 8), CHUNK)
                for lt in range(LT):
                    v = r[rows, :, pl.ds(lt * 128, 128)].astype(jnp.float32)
                    s[:, lt, rows, :] = jnp.swapaxes(v, 0, 1)
                return 0

            lax.fori_loop(0, D, turn, 0)

        def square(c):
            return jnp.concatenate([s[c, lt] for lt in range(LT)], axis=1).astype(jnp.bfloat16)

        def contract(c, dims):
            prod = lax.dot_general(square(c), square(c + CPD), (dims, ((), ())), preferred_element_type=jnp.float32)
            for lt in range(LT):
                t[c, lt] = prod[:, lt * 128:(lt + 1) * 128]

        @pl.when(u % 2 == 0)
        def _():
            def one(c, _):
                contract(c, ((1,), (1,)))
                return 0
            lax.fori_loop(0, CPD, one, 0)

        @pl.when(u % 2 == 1)
        def _():
            def one(c, _):
                contract(c, ((0,), (0,)))
                return 0
            lax.fori_loop(0, CPD, one, 0)

        def give(d, _):
            dst, num = place(d)
            for k in range(NCHUNK):
                rows = pl.ds(pl.multiple_of(num * ROWS + k * 8, 8), 8)
                pairs = pl.ds(num * (ROWS // 2) + k * 4, 4)
                for lt in range(LT):
                    v = jnp.swapaxes(t[:, lt, rows, :], 0, 1)
                    tsend[pairs, :, pl.ds(lt * 128, 128)] = v.reshape(4, 16, 128).astype(jnp.bfloat16)
            pairs = pl.ds(num * (ROWS // 2), ROWS // 2)

            @pl.when(d > 0)
            def _():
                pltpu.make_async_remote_copy(tsend.at[pairs], trecv.at[me], tsend_sem, trecv_sem,
                                             device_id=dst, device_id_type=MESH).start()

            @pl.when(d == 0)
            def _():
                trecv[me] = tsend[pairs]
            return 0

        lax.fori_loop(0, D, give, 0)
        part = trecv.at[pl.ds(0, D - 1)]
        pltpu.make_async_copy(part, part, trecv_sem).wait()
        part = ab.at[pl.ds(0, D - 1)]
        pltpu.make_async_copy(part, part, absend_sem).wait()
        part = tsend.at[pl.ds(0, (D - 1) * (ROWS // 2))]
        pltpu.make_async_copy(part, part, tsend_sem).wait()

        for c in range(NCHUNK):
            def one(p, _):
                finish(u, c * (CHUNK // 2) + p)
                return 0

            lax.fori_loop(0, CHUNK // 2, one, 0)

            @pl.when(u < UPDATES - 1)
            def _():
                project_chunk(jnp.minimum(u + 1, UPDATES - 1), c)
        return 0

    lax.fori_loop(0, UPDATES, update, 0)

    def turn_out(i, _):
        zrow[i] = z[i].T
        return 0

    lax.fori_loop(0, ROWS, turn_out, 0)

    home = 2 * g + zl
    mine = pl.ds(pl.multiple_of(iy * ROWS, 8), ROWS)

    def blocks_back(j, start):
        here = jnp.logical_and(jnp.logical_and(half == g, jz == j), iy == home)
        src = zrow.at[:, pl.ds(j * BLK, BLK), :]
        dst_ref = out.at[mine]

        @pl.when(jnp.logical_not(here))
        def _():
            copy = pltpu.make_async_remote_copy(src, dst_ref, osend_sem.at[j], orecv_sem,
                                                device_id=(half, j, home), device_id_type=MESH)
            if start:
                copy.start()
            else:
                copy.wait_send()

        if start:
            @pl.when(here)
            def _():
                pltpu.make_async_copy(src, dst_ref, orecv_sem).start()

    for j in range(4):
        blocks_back(j, True)
    pltpu.make_async_copy(out, out, orecv_sem).wait()
    for j in range(4):
        blocks_back(j, False)


def local_fn(pair_act, pair_mask, in_gamma, in_beta, w_proj, w_gate, out_gamma, out_beta, w_out):
    mask = jnp.pad(pair_mask.astype(jnp.float32), ((0, 0), (0, 128 - BLK)))

    def spread(v):
        return jnp.broadcast_to(v.reshape(UPDATES, C, 1), (UPDATES, C, 128))

    def turned(w):
        return jnp.swapaxes(w.reshape((UPDATES,) + w.shape[2:]), 1, 2)

    any_spec = pl.BlockSpec(memory_space=pl.ANY)
    vmem = pl.BlockSpec(memory_space=pltpu.VMEM)
    bf16, f32 = jnp.bfloat16, jnp.float32
    return pl.pallas_call(
        kernel,
        out_shape=jax.ShapeDtypeStruct((BLK, BLK, C), bf16),
        in_specs=[any_spec, any_spec] + [vmem] * 7,
        out_specs=any_spec,
        scratch_shapes=[
            pltpu.VMEM((ROWS, N, C), bf16),
            pltpu.VMEM((4, ROWS, 128), f32),
            pltpu.VMEM((ROWS, N), f32),
            pltpu.VMEM((ROWS, C, N), bf16),
            pltpu.VMEM((ROWS, C, N), f32),
            pltpu.VMEM((C, 2 * N), bf16),
            pltpu.VMEM((5 * C, 2 * N), f32),
            pltpu.VMEM((C, 2 * N), bf16),
            pltpu.VMEM((D, ROWS, 2 * CPD, N), bf16),
            pltpu.VMEM((N, 2 * CPD, N), bf16),
            pltpu.VMEM((2 * CPD, LT, N, 128), f32),
            pltpu.VMEM((CPD, LT, N, 128), f32),
            pltpu.VMEM((N // 2, 2 * CPD, N), bf16),
            pltpu.VMEM((D, ROWS // 2, 2 * CPD, N), bf16),
            pltpu.SemaphoreType.DMA((4,)),
            pltpu.SemaphoreType.DMA((4,)),
            pltpu.SemaphoreType.DMA,
            pltpu.SemaphoreType.DMA,
            pltpu.SemaphoreType.DMA,
            pltpu.SemaphoreType.DMA((NCHUNK,)),
            pltpu.SemaphoreType.DMA,
            pltpu.SemaphoreType.DMA,
            pltpu.SemaphoreType.DMA((4,)),
            pltpu.SemaphoreType.DMA,
        ],
        compiler_params=pltpu.CompilerParams(has_side_effects=True, vmem_limit_bytes=60 * 1024 * 1024),
        name="triangle",
    )(pair_act, mask, spread(in_gamma), spread(in_beta), turned(w_proj), turned(w_gate),
      spread(out_gamma), spread(out_beta), turned(w_out))


def solution(mesh):
    pair_spec = P(("data", "dap"), "dap2", None)
    mask_spec = P(("data", "dap"), "dap2")
    return jax.shard_map(local_fn, mesh=mesh, in_specs=(pair_spec, mask_spec) + (P(),) * 7,
                         out_specs=pair_spec, check_vma=False)
```

time: 3020 us -> 947 us (0.31)
  waiting for transfers between devices: 1810 us -> 0 us
  Pallas kernels: 0 us -> 931 us
  local copies, waits for them, and re-layouts: 464 us -> 14.8 us
  blocking collectives: 248 us -> 0 us
  starting transfers between devices: 241 us -> 0 us
  other arithmetic: 132 us -> 0.89 us
  matrix products: 96.7 us -> 0 us
    all_to_all x40 -> x0, waiting for transfers between devices: 1810 us -> none  [the longest x16 934 us: to_channels(): col_full = lax.all_to_all(block, 'dap2', 0, 2, tiled=True)]
    pallas_call x0 -> x1, Pallas kernels: none -> 931 us  [local_fn(): pl.pallas_call(kernel, out_shape=jax.ShapeDtypeStruct((BLK, BLK, C), bf16...]
    all_to_all x72 -> x0, local copies, waits for them, and re-layouts: 272 us -> none  [the longest x32 178 us: to_channels(): col_full = lax.all_to_all(block, 'dap2', 0, 2, tiled=True)]
    all_to_all x8 -> x0, blocking collectives: 248 us -> none  [from_channels(): row_part = lax.all_to_all(block, 'dap', 1, 0, tiled=True)]
    all_to_all x40 -> x0, starting transfers between devices: 241 us -> none  [the longest x16 110 us: to_channels(): col_full = lax.all_to_all(block, 'dap2', 0, 2, tiled=True)]
    convert_element_type x40 -> x0, local copies, waits for them, and re-layouts: 164 us -> none  [the longest x8 59.3 us: finish_local(): tri_blk.astype(jnp.float32)]
    dot_general x32 -> x0, matrix products: 96.7 us -> none  [the longest x8 46.8 us: project_local(): jnp.einsum('ijd,de->ije', normed, w_gate, preferred_element_type=jnp.floa...]
    reduce_sum x25 -> x0, other arithmetic: 81.5 us -> none  [the longest x16 43.4 us: layer_norm(): variance = jnp.mean(centered * centered, axis=axis, keepdims=True)]
  transfers between devices with their start and end apart: 40 -> 0, of which waited for: 40 -> 0; matrix products, arithmetic and copies ran while one was open for 5% -> 0% of each run, Pallas kernels for 0% -> 0%
where the time goes in v1:
time: 947 us; the launch traced here: 946 us
  Pallas kernels  931 us (98%)
  local copies, waits for them, and re-layouts  14.8 us (2%)
    pallas_call x1, Pallas kernels, local_fn(): pl.pallas_call(kernel, out_shape=jax.ShapeDtypeStruct((BLK, BLK, C), bf16...  931 us

profile of v1, /device:TPU:10, one launch (start us, length us, event | category | flops | bytes accessed | tf_op | source)
XLA Modules:
  0.0 946.2 jit_solution(1958033814296106418)
XLA Ops:
  0.0 0.0 copy-start.1
  0.0 0.0 copy-start
  0.0 0.9 convert_element_type.5
  0.9 0.6 pad.4.m_in
  1.5 1.8 copy.11
  3.3 1.8 copy.12
  5.1 1.7 broadcast_in_dim.29.gin
  6.8 1.7 broadcast_in_dim.31.bin_
  8.5 1.7 broadcast_in_dim.33.gout
  10.2 0.0 copy-done.1
  10.2 1.0 broadcast_in_dim.35.bout
  11.2 0.0 copy-done
  11.2 1.3 copy.10
  12.5 930.5 %triangle.1 = bf16[96,96,128]{2,1,0:T(8,128)(2,1)} custom-call(bf16[96,96,128]{2,1,0:T(8,128)(2,1)} %z_in.1, f32[96,128]{1,0:T(8,128)} %pad.4.m_in, f32[8,128,128]{2,1,0:T(8,128)} %broadcast_in_dim.29.gin, f32[8,128,128]{2,1,0:T(8,128)} %broadcast_in_dim.31.bin_, bf16[8,512,128]{2,1,0:T(8,128)(2,1)} %bitcast.13, bf16[8,128,128]{2,1,0:T(8,128)(2,1)} %bitcast.14, ...), custom_call_target="tpu_custom_call" | custom-call | tf_op jit(solution)/shard_map/triangle/pallas_call | solution.py:277
  943.0 3.2 copy.14
Async XLA Ops:
  0.0 10.2 %copy-start.1 = (f32[4,2,128]{2,1,0:T(2,128)S(1)}, f32[4,2,128]{2,1,0:T(2,128)}, u32[]{:S(2)}) copy-start(f32[4,2,128]{2,1,0:T(2,128)} %param.16) | copy-start | bytes 12292
  0.0 11.2 %copy-start = (bf16[4,2,128,512]{3,2,1,0:T(8,128)(2,1)S(1)}, bf16[4,2,128,512]{3,2,1,0:T(8,128)(2,1)}, u32[]{:S(2)}) copy-start(bf16[4,2,128,512]{3,2,1,0:T(8,128)(2,1)} %param.13) | copy-start | bytes 3145732

commit v2 on v1

--- a/solution.py
+++ b/solution.py
@@ -34,48 +34,104 @@
 
 def kernel(z_in, m_in, gin, bin_, wp, wg, gout, bout, wo, out,
            zrow, mrow, mask, z, gate, x, q, y, ab, r, s, t, tsend, trecv,
-           zsend_sem, msend_sem, zrecv_sem, mrecv_sem, absend_sem, abrecv_sem, tsend_sem, trecv_sem,
-           osend_sem, orecv_sem):
+           relay, zsend_sem, msend_sem, fsend_sem, zrecv_sem, mrecv_sem, lrecv_sem, absend_sem, abrecv_sem,
+           tsend_sem, trecv_sem, osend_sem, orecv_sem):
     g = lax.axis_index("data")
     jz = lax.axis_index("dap2")
     iy = lax.axis_index("dap")
     half = jz // 2
     zl = jz % 2
-    me = g * 8 + zl * 4 + iy
+    core = iy % 2
+    me = iy * 4 + g * 2 + zl
     row0 = me * ROWS
 
-    def place(d):
-        px = (g + d // 8) % 2
-        pz = (zl + (d // 4) % 2) % 2
-        py = (iy + d % 4) % 4
-        return (px, 2 * half + pz, py), px * 8 + pz * 4 + py
-
-    def blocks_out(q_, start):
-        here = jnp.logical_and(jnp.logical_and(iy // 2 == g, jz == 2 * g + iy % 2), iy == q_)
-        dst = (iy // 2, 2 * g + iy % 2, q_)
-        rows = pl.ds(q_ * ROWS, ROWS)
-        cols = pl.ds(pl.multiple_of(jz * BLK, 32), BLK)
-        for src, dst_ref, send, recv in (
-            (z_in.at[rows], zrow.at[:, cols, :], zsend_sem.at[q_], zrecv_sem),
-            (m_in.at[rows], mrow.at[jz], msend_sem.at[q_], mrecv_sem),
-        ):
-            @pl.when(jnp.logical_not(here))
-            def _():
-                copy = pltpu.make_async_remote_copy(src, dst_ref, send, recv, device_id=dst, device_id_type=MESH)
-                if start:
-                    copy.start()
-                else:
-                    copy.wait_send()
-
+    def place(n):
+        k = n // 2
+        dz = 1 - n % 2
+        step = (k + 2 * core) % 4
+        lo = 1 - k // 6
+        dy = dz * (1 - step // 2) + (1 - dz) * (1 - (k % 3) // 2) * lo
+        dx = dz * (((step + 1) // 2) % 2) + (1 - dz) * (((k % 3 + 1) // 2) * lo + core * dy) % 2
+        dc = dz * (k // 4) + (1 - dz) * (lo * (k // 3) + (1 - lo) * (1 - k % 2))
+        px = (g + dx) % 2
+        pz = (zl + dz) % 2
+        py = ((iy // 2 + dy) % 2) * 2 + (core + dc) % 2
+        return (px, 2 * half + pz, py), py * 4 + px * 2 + pz
+
+    def cols(j):
+        return pl.ds(pl.multiple_of(j * BLK, 32), BLK)
+
+    def block_out(q_, c, start):
+        px, pz = q_ // 2, 2 * g + q_ % 2
+        rows = pl.ds(c * CHUNK, CHUNK)
+        src = z_in.at[pl.ds(q_ * ROWS + c * CHUNK, CHUNK)]
+        into = zrow.at[rows, cols(jz), :]
+        stay = px == g
+        there = pz == jz
+
+        def go(copy):
             if start:
-                @pl.when(here)
-                def _():
-                    pltpu.make_async_copy(src, dst_ref, recv).start()
+                copy.start()
+            else:
+                copy.wait_send()
+
+        @pl.when(jnp.logical_or(jnp.logical_and(stay, jnp.logical_not(there)), jnp.logical_and(jnp.logical_not(stay), there)))
+        def _():
+            go(pltpu.make_async_remote_copy(src, into, zsend_sem.at[q_, c], zrecv_sem.at[c],
+                                            device_id=(px, pz, iy), device_id_type=MESH))
+
+        @pl.when(jnp.logical_and(jnp.logical_not(stay), jnp.logical_not(there)))
+        def _():
+            go(pltpu.make_async_remote_copy(src, relay.at[q_ % 2, rows], zsend_sem.at[q_, c], lrecv_sem.at[q_ % 2, c],
+                                            device_id=(px, jz, iy), device_id_type=MESH))
+
+        if start:
+            @pl.when(jnp.logical_and(stay, there))
+            def _():
+                pltpu.make_async_copy(src, into, zrecv_sem.at[c]).start()
+
+    def pass_on(zq, c, start):
+        rows = pl.ds(c * CHUNK, CHUNK)
+        pz = 2 * (1 - g) + zq
+
+        @pl.when(pz != jz)
+        def _():
+            copy = pltpu.make_async_remote_copy(relay.at[zq, rows], zrow.at[rows, cols(jz), :], fsend_sem.at[zq, c],
+                                                zrecv_sem.at[c], device_id=(g, pz, iy), device_id_type=MESH)
+            if start:
+                got = relay.at[zq, rows]
+                pltpu.make_async_copy(got, got, lrecv_sem.at[zq, c]).wait()
+                copy.start()
+            else:
+                copy.wait_send()
+
+    def mask_out(q_, start):
+        here = jnp.logical_and(q_ // 2 == g, jz == 2 * g + q_ % 2)
+        src = m_in.at[pl.ds(q_ * ROWS, ROWS)]
+
+        @pl.when(jnp.logical_not(here))
+        def _():
+            copy = pltpu.make_async_remote_copy(src, mrow.at[jz], msend_sem.at[q_], mrecv_sem,
+                                                device_id=(q_ // 2, 2 * g + q_ % 2, iy), device_id_type=MESH)
+            if start:
+                copy.start()
+            else:
+                copy.wait_send()
+
+        if start:
+            @pl.when(here)
+            def _():
+                pltpu.make_async_copy(src, mrow.at[jz], mrecv_sem).start()
 
     for q_ in range(4):
-        blocks_out(q_, True)
+        mask_out(q_, True)
+    for c in range(NCHUNK):
+        for q_ in range(4):
+            block_out(q_, c, True)
+    for c in range(NCHUNK):
+        for zq in range(2):
+            pass_on(zq, c, True)
     pltpu.make_async_copy(mrow, mrow, mrecv_sem).wait()
-    pltpu.make_async_copy(zrow, zrow, zrecv_sem).wait()
     lane = lax.broadcasted_iota(jnp.int32, (128, N), 0)
     col = lax.broadcasted_iota(jnp.int32, (128, N), 1)
     total = jnp.zeros((ROWS, N), jnp.float32)
@@ -83,14 +139,6 @@
         pick = jnp.logical_and(col == lane + j * BLK, lane < BLK).astype(jnp.float32)
         total = total + jnp.dot(mrow[j], pick, preferred_element_type=jnp.float32)
     mask[...] = total
-    for q_ in range(4):
-        blocks_out(q_, False)
-
-    def turn_in(i, _):
-        z[i] = zrow[i].T
-        return 0
-
-    lax.fori_loop(0, ROWS, turn_in, 0)
 
     def project(u, p):
         for h in range(2):
@@ -135,7 +183,7 @@
                                          device_id=dst, device_id_type=MESH).start()
             return 0
 
-        lax.fori_loop(1, D, to, 0)
+        lax.fori_loop(0, D - 1, to, 0)
         r[mine] = ab[me, rows]
 
     def project_chunk(u, c):
@@ -147,7 +195,41 @@
         send_ab(c)
 
     for c in range(NCHUNK):
+        got = zrow.at[pl.ds(c * CHUNK, CHUNK)]
+        pltpu.make_async_copy(got, got, zrecv_sem.at[c]).wait()
+
+        def turn_in(i, _):
+            z[c * CHUNK + i] = zrow[c * CHUNK + i].T
+            return 0
+
+        lax.fori_loop(0, CHUNK, turn_in, 0)
         project_chunk(0, c)
+    for q_ in range(4):
+        mask_out(q_, False)
+        for c in range(NCHUNK):
+            block_out(q_, c, False)
+    for c in range(NCHUNK):
+        for zq in range(2):
+            pass_on(zq, c, False)
+
+    def block_back(j, c, start):
+        here = jnp.logical_and(half == g, jz == j)
+        src = zrow.at[pl.ds(c * CHUNK, CHUNK), pl.ds(j * BLK, BLK), :]
+        into = out.at[pl.ds(pl.multiple_of((2 * g + zl) * ROWS + c * CHUNK, 8), CHUNK)]
+
+        @pl.when(jnp.logical_not(here))
+        def _():
+            copy = pltpu.make_async_remote_copy(src, into, osend_sem.at[j, c], orecv_sem,
+                                                device_id=(half, j, iy), device_id_type=MESH)
+            if start:
+                copy.start()
+            else:
+                copy.wait_send()
+
+        if start:
+            @pl.when(here)
+            def _():
+                pltpu.make_async_copy(src, into, orecv_sem).start()
 
     def update(u, _):
         for c in range(NCHUNK):
@@ -185,81 +267,64 @@
                 return 0
             lax.fori_loop(0, CPD, one, 0)
 
-        def give(d, _):
-            dst, num = place(d)
-            for k in range(NCHUNK):
-                rows = pl.ds(pl.multiple_of(num * ROWS + k * 8, 8), 8)
-                pairs = pl.ds(num * (ROWS // 2) + k * 4, 4)
+        for c in range(NCHUNK):
+            def give(n, _):
+                dst, num = place(n)
+                rows = pl.ds(pl.multiple_of(num * ROWS + c * CHUNK, 8), CHUNK)
+                pairs = pl.ds(num * (ROWS // 2) + c * (CHUNK // 2), CHUNK // 2)
+                into = pl.ds(c * (CHUNK // 2), CHUNK // 2)
                 for lt in range(LT):
                     v = jnp.swapaxes(t[:, lt, rows, :], 0, 1)
-                    tsend[pairs, :, pl.ds(lt * 128, 128)] = v.reshape(4, 16, 128).astype(jnp.bfloat16)
-            pairs = pl.ds(num * (ROWS // 2), ROWS // 2)
-
-            @pl.when(d > 0)
-            def _():
-                pltpu.make_async_remote_copy(tsend.at[pairs], trecv.at[me], tsend_sem, trecv_sem,
-                                             device_id=dst, device_id_type=MESH).start()
-
-            @pl.when(d == 0)
-            def _():
-                trecv[me] = tsend[pairs]
-            return 0
-
-        lax.fori_loop(0, D, give, 0)
-        part = trecv.at[pl.ds(0, D - 1)]
-        pltpu.make_async_copy(part, part, trecv_sem).wait()
-        part = ab.at[pl.ds(0, D - 1)]
-        pltpu.make_async_copy(part, part, absend_sem).wait()
+                    tsend[pairs, :, pl.ds(lt * 128, 128)] = v.reshape(CHUNK // 2, 16, 128).astype(jnp.bfloat16)
+
+                @pl.when(n < D - 1)
+                def _():
+                    pltpu.make_async_remote_copy(tsend.at[pairs], trecv.at[me, into], tsend_sem, trecv_sem.at[c],
+                                                 device_id=dst, device_id_type=MESH).start()
+
+                @pl.when(n == D - 1)
+                def _():
+                    trecv[me, into] = tsend[pairs]
+                return 0
+
+            lax.fori_loop(0, D, give, 0)
+
+        for c in range(NCHUNK):
+            part = tsend.at[pl.ds(0, (D - 1) * (CHUNK // 2))]
+            pltpu.make_async_copy(part, part, trecv_sem.at[c]).wait()
+            if c == 0:
+                part = ab.at[pl.ds(0, D - 1)]
+                pltpu.make_async_copy(part, part, absend_sem).wait()
+
+            def one(p, _):
+                finish(u, c * (CHUNK // 2) + p)
+                return 0
+
+            lax.fori_loop(0, CHUNK // 2, one, 0)
+
+            @pl.when(u < UPDATES - 1)
+            def _():
+                project_chunk(jnp.minimum(u + 1, UPDATES - 1), c)
+
+            @pl.when(u == UPDATES - 1)
+            def _():
+                def turn_out(i, _):
+                    zrow[c * CHUNK + i] = z[c * CHUNK + i].T
+                    return 0
+
+                lax.fori_loop(0, CHUNK, turn_out, 0)
+                for j in range(4):
+                    block_back(j, c, True)
         part = tsend.at[pl.ds(0, (D - 1) * (ROWS // 2))]
         pltpu.make_async_copy(part, part, tsend_sem).wait()
-
-        for c in range(NCHUNK):
-            def one(p, _):
-                finish(u, c * (CHUNK // 2) + p)
-                return 0
-
-            lax.fori_loop(0, CHUNK // 2, one, 0)
-
-            @pl.when(u < UPDATES - 1)
-            def _():
-                project_chunk(jnp.minimum(u + 1, UPDATES - 1), c)
         return 0
 
     lax.fori_loop(0, UPDATES, update, 0)
 
-    def turn_out(i, _):
-        zrow[i] = z[i].T
-        return 0
-
-    lax.fori_loop(0, ROWS, turn_out, 0)
-
-    home = 2 * g + zl
-    mine = pl.ds(pl.multiple_of(iy * ROWS, 8), ROWS)
-
-    def blocks_back(j, start):
-        here = jnp.logical_and(jnp.logical_and(half == g, jz == j), iy == home)
-        src = zrow.at[:, pl.ds(j * BLK, BLK), :]
-        dst_ref = out.at[mine]
-
-        @pl.when(jnp.logical_not(here))
-        def _():
-            copy = pltpu.make_async_remote_copy(src, dst_ref, osend_sem.at[j], orecv_sem,
-                                                device_id=(half, j, home), device_id_type=MESH)
-            if start:
-                copy.start()
-            else:
-                copy.wait_send()
-
-        if start:
-            @pl.when(here)
-            def _():
-                pltpu.make_async_copy(src, dst_ref, orecv_sem).start()
-
-    for j in range(4):
-        blocks_back(j, True)
     pltpu.make_async_copy(out, out, orecv_sem).wait()
-    for j in range(4):
-        blocks_back(j, False)
+    for c in range(NCHUNK):
+        for j in range(4):
+            block_back(j, c, False)
 
 
 def local_fn(pair_act, pair_mask, in_gamma, in_beta, w_proj, w_gate, out_gamma, out_beta, w_out):
@@ -294,15 +359,18 @@
             pltpu.VMEM((CPD, LT, N, 128), f32),
             pltpu.VMEM((N // 2, 2 * CPD, N), bf16),
             pltpu.VMEM((D, ROWS // 2, 2 * CPD, N), bf16),
+            pltpu.VMEM((2, ROWS, BLK, C), bf16),
+            pltpu.SemaphoreType.DMA((4, NCHUNK)),
             pltpu.SemaphoreType.DMA((4,)),
-            pltpu.SemaphoreType.DMA((4,)),
+            pltpu.SemaphoreType.DMA((2, NCHUNK)),
+            pltpu.SemaphoreType.DMA((NCHUNK,)),
             pltpu.SemaphoreType.DMA,
-            pltpu.SemaphoreType.DMA,
+            pltpu.SemaphoreType.DMA((2, NCHUNK)),
             pltpu.SemaphoreType.DMA,
             pltpu.SemaphoreType.DMA((NCHUNK,)),
             pltpu.SemaphoreType.DMA,
-            pltpu.SemaphoreType.DMA,
-            pltpu.SemaphoreType.DMA((4,)),
+            pltpu.SemaphoreType.DMA((NCHUNK,)),
+            pltpu.SemaphoreType.DMA((4, NCHUNK)),
             pltpu.SemaphoreType.DMA,
         ],
         compiler_params=pltpu.CompilerParams(has_side_effects=True, vmem_limit_bytes=60 * 1024 * 1024),

time: 947 us -> 785 us (0.83)
  Pallas kernels: 931 us -> 769 us
    pallas_call x1, Pallas kernels: 931 us -> 769 us  [local_fn(): pl.pallas_call(kernel, out_shape=jax.ShapeDtypeStruct((BLK, BLK, C), bf16...]
where the time goes in v2:
time: 785 us
  Pallas kernels  769 us (98%)
  local copies, waits for them, and re-layouts  14.8 us (2%)
    pallas_call x1, Pallas kernels, local_fn(): pl.pallas_call(kernel, out_shape=jax.ShapeDtypeStruct((BLK, BLK, C), bf16...  769 us

profile of v2, /device:TPU:10, one launch (start us, length us, event | category | flops | bytes accessed | tf_op | source)
XLA Modules:
  0.0 784.7 jit_solution(963539898720225400)
XLA Ops:
  0.0 0.0 copy-start.1
  0.0 0.0 copy-start
  0.0 0.9 convert_element_type.5
  0.9 0.6 pad.4.m_in
  1.5 1.8 copy.11
  3.3 1.8 copy.12
  5.1 1.7 broadcast_in_dim.29.gin
  6.8 1.7 broadcast_in_dim.31.bin_
  8.5 1.7 broadcast_in_dim.33.gout
  10.2 0.0 copy-done.1
  10.2 1.0 broadcast_in_dim.35.bout
  11.2 0.0 copy-done
  11.2 1.3 copy.10
  12.5 769.0 %triangle.1 = bf16[96,96,128]{2,1,0:T(8,128)(2,1)} custom-call(bf16[96,96,128]{2,1,0:T(8,128)(2,1)} %z_in.1, f32[96,128]{1,0:T(8,128)} %pad.4.m_in, f32[8,128,128]{2,1,0:T(8,128)} %broadcast_in_dim.29.gin, f32[8,128,128]{2,1,0:T(8,128)} %broadcast_in_dim.31.bin_, bf16[8,512,128]{2,1,0:T(8,128)(2,1)} %bitcast.13, bf16[8,128,128]{2,1,0:T(8,128)(2,1)} %bitcast.14, ...), custom_call_target="tpu_custom_call" | custom-call | tf_op jit(solution)/shard_map/triangle/pallas_call | solution.py:342
  781.5 3.2 copy.14
Async XLA Ops:
  0.0 10.2 %copy-start.1 = (f32[4,2,128]{2,1,0:T(2,128)S(1)}, f32[4,2,128]{2,1,0:T(2,128)}, u32[]{:S(2)}) copy-start(f32[4,2,128]{2,1,0:T(2,128)} %param.16) | copy-start | bytes 12292
  0.0 11.2 %copy-start = (bf16[4,2,128,512]{3,2,1,0:T(8,128)(2,1)S(1)}, bf16[4,2,128,512]{3,2,1,0:T(8,128)(2,1)}, u32[]{:S(2)}) copy-start(bf16[4,2,128,512]{3,2,1,0:T(8,128)(2,1)} %param.13) | copy-start | bytes 3145732

commit v3 on v2

--- a/solution.py
+++ b/solution.py
@@ -32,8 +32,8 @@
     return centered * lax.rsqrt(variance + NORM_EPS) * gamma + beta
 
 
-def kernel(z_in, m_in, gin, bin_, wp, wg, gout, bout, wo, out,
-           zrow, mrow, mask, z, gate, x, q, y, ab, r, s, t, tsend, trecv,
+def kernel(z_in, m_in, gin_in, bin_in, wp_in, wg_in, gout_in, bout_in, wo_in, out,
+           wp, wg, wo, gin, bin_, gout, bout, msend, zrow, mrow, mask, z, gate, x, q, y, ab, r, s, t, tsend, trecv,
            relay, zsend_sem, msend_sem, fsend_sem, zrecv_sem, mrecv_sem, lrecv_sem, absend_sem, abrecv_sem,
            tsend_sem, trecv_sem, osend_sem, orecv_sem):
     g = lax.axis_index("data")
@@ -43,7 +43,6 @@
     zl = jz % 2
     core = iy % 2
     me = iy * 4 + g * 2 + zl
-    row0 = me * ROWS
 
     def place(n):
         k = n // 2
@@ -107,7 +106,8 @@
 
     def mask_out(q_, start):
         here = jnp.logical_and(q_ // 2 == g, jz == 2 * g + q_ % 2)
-        src = m_in.at[pl.ds(q_ * ROWS, ROWS)]
+        rows = pl.ds(q_ * ROWS, ROWS)
+        src = msend.at[rows]
 
         @pl.when(jnp.logical_not(here))
         def _():
@@ -121,22 +121,39 @@
         if start:
             @pl.when(here)
             def _():
-                pltpu.make_async_copy(src, mrow.at[jz], mrecv_sem).start()
-
-    for q_ in range(4):
-        mask_out(q_, True)
+                mrow[jz] = msend[rows]
+
     for c in range(NCHUNK):
         for q_ in range(4):
             block_out(q_, c, True)
+    msend[...] = jnp.zeros_like(msend)
+    msend[:, pl.ds(0, BLK)] = m_in[...].astype(jnp.float32)
+    for q_ in range(4):
+        mask_out(q_, True)
+
+    def prepare(u, _):
+        wp[u] = wp_in[u].T
+        wg[u] = wg_in[u].T
+        wo[u] = wo_in[u].T
+        for src, dst in ((gin_in, gin), (bin_in, bin_), (gout_in, gout), (bout_in, bout)):
+            dst[u] = jnp.broadcast_to(src[u // 2, pl.ds(u % 2, 1), :], (C, C)).T
+        return 0
+
+    lax.fori_loop(0, UPDATES, prepare, 0)
     for c in range(NCHUNK):
         for zq in range(2):
             pass_on(zq, c, True)
-    pltpu.make_async_copy(mrow, mrow, mrecv_sem).wait()
+    for n_from in (3, 4):
+        @pl.when((n_from == 3) == (half == g))
+        def _():
+            part = mrow.at[pl.ds(0, n_from)]
+            pltpu.make_async_copy(part, part, mrecv_sem).wait()
     lane = lax.broadcasted_iota(jnp.int32, (128, N), 0)
     col = lax.broadcasted_iota(jnp.int32, (128, N), 1)
+    natural = (col % 128) // CHUNK * ROWS + col // 128 * CHUNK + col % CHUNK
     total = jnp.zeros((ROWS, N), jnp.float32)
     for j in range(4):
-        pick = jnp.logical_and(col == lane + j * BLK, lane < BLK).astype(jnp.float32)
+        pick = jnp.logical_and(natural == lane + j * BLK, lane < BLK).astype(jnp.float32)
         total = total + jnp.dot(mrow[j], pick, preferred_element_type=jnp.float32)
     mask[...] = total
 
@@ -174,7 +191,7 @@
                 z[2 * p + h, rows, :] = (z[2 * p + h, rows, :].astype(jnp.float32) + upd).astype(jnp.bfloat16)
 
     def send_ab(c):
-        mine = pl.ds(pl.multiple_of(row0 + c * CHUNK, 8), CHUNK)
+        mine = pl.ds(pl.multiple_of(c * 128 + me * CHUNK, 8), CHUNK)
         rows = pl.ds(c * CHUNK, CHUNK)
 
         def to(d, _):
@@ -199,7 +216,10 @@
         pltpu.make_async_copy(got, got, zrecv_sem.at[c]).wait()
 
         def turn_in(i, _):
-            z[c * CHUNK + i] = zrow[c * CHUNK + i].T
+            v = zrow[c * CHUNK + i].astype(jnp.float32)
+            v = jnp.concatenate([v[k * ROWS + e * CHUNK:k * ROWS + (e + 1) * CHUNK]
+                                 for e in range(NCHUNK) for k in range(D)], axis=0)
+            z[c * CHUNK + i] = v.T.astype(jnp.bfloat16)
             return 0
 
         lax.fori_loop(0, CHUNK, turn_in, 0)
@@ -232,45 +252,67 @@
                 pltpu.make_async_copy(src, into, orecv_sem).start()
 
     def update(u, _):
+        def block(ch, c, lts=range(LT)):
+            rows = pl.ds(c * 128, 128)
+            return jnp.concatenate([s[ch, lt, rows, :] for lt in lts], axis=1).astype(jnp.bfloat16)
+
+        def dot(lhs, rhs, dim):
+            return lax.dot_general(lhs, rhs, (((dim,), (dim,)), ((), ())), preferred_element_type=jnp.float32)
+
+        def outer(rows, lts):
+            def one(ch, _):
+                right = [block(ch + CPD, lt) for lt in lts]
+                right = jnp.concatenate(right, axis=0)
+                for i in rows:
+                    prod = dot(block(ch, i), right, 1)
+                    for n, lt in enumerate(lts):
+                        t[ch, lt, pl.ds(i * 128, 128), :] = prod[:, n * 128:(n + 1) * 128]
+                return 0
+
+            @pl.when(u % 2 == 0)
+            def _():
+                lax.fori_loop(0, CPD, one, 0)
+
+        def inner(rows, c):
+            def one(ch, _):
+                right = block(ch + CPD, c)
+                for i in rows:
+                    prod = dot(block(ch, c, (i,)), right, 0)
+                    for lt in range(LT):
+                        at = pl.ds(i * 128, 128)
+                        part = prod[:, lt * 128:(lt + 1) * 128]
+                        t[ch, lt, at, :] = part if c == 0 else t[ch, lt, at, :] + part
+                return 0
+
+            @pl.when(u % 2 == 1)
+            def _():
+                lax.fori_loop(0, CPD, one, 0)
+
         for c in range(NCHUNK):
             part = r.at[pl.ds(0, (D - 1) * CHUNK)]
             pltpu.make_async_copy(part, part, abrecv_sem.at[c]).wait()
 
             def turn(k, _):
-                rows = pl.ds(pl.multiple_of(k * ROWS + c * CHUNK, 8), CHUNK)
+                rows = pl.ds(pl.multiple_of(c * 128 + k * CHUNK, 8), CHUNK)
                 for lt in range(LT):
                     v = r[rows, :, pl.ds(lt * 128, 128)].astype(jnp.float32)
                     s[:, lt, rows, :] = jnp.swapaxes(v, 0, 1)
                 return 0
 
             lax.fori_loop(0, D, turn, 0)
-
-        def square(c):
-            return jnp.concatenate([s[c, lt] for lt in range(LT)], axis=1).astype(jnp.bfloat16)
-
-        def contract(c, dims):
-            prod = lax.dot_general(square(c), square(c + CPD), (dims, ((), ())), preferred_element_type=jnp.float32)
-            for lt in range(LT):
-                t[c, lt] = prod[:, lt * 128:(lt + 1) * 128]
-
-        @pl.when(u % 2 == 0)
-        def _():
-            def one(c, _):
-                contract(c, ((1,), (1,)))
-                return 0
-            lax.fori_loop(0, CPD, one, 0)
-
-        @pl.when(u % 2 == 1)
-        def _():
-            def one(c, _):
-                contract(c, ((0,), (0,)))
-                return 0
-            lax.fori_loop(0, CPD, one, 0)
-
+            if c < NCHUNK - 1:
+                outer(range(c), (c,))
+                outer((c,), range(c + 1))
+                inner(range(LT), c)
+
+        last = NCHUNK - 1
         for c in range(NCHUNK):
+            outer((c,), range(NCHUNK) if c == last else (last,))
+            inner((c,), last)
+
             def give(n, _):
                 dst, num = place(n)
-                rows = pl.ds(pl.multiple_of(num * ROWS + c * CHUNK, 8), CHUNK)
+                rows = pl.ds(pl.multiple_of(c * 128 + num * CHUNK, 8), CHUNK)
                 pairs = pl.ds(num * (ROWS // 2) + c * (CHUNK // 2), CHUNK // 2)
                 into = pl.ds(c * (CHUNK // 2), CHUNK // 2)
                 for lt in range(LT):
@@ -309,7 +351,10 @@
             @pl.when(u == UPDATES - 1)
             def _():
                 def turn_out(i, _):
-                    zrow[c * CHUNK + i] = z[c * CHUNK + i].T
+                    v = z[c * CHUNK + i].astype(jnp.float32).T
+                    v = jnp.concatenate([v[e * 128 + k * CHUNK:e * 128 + (k + 1) * CHUNK]
+                                         for k in range(D) for e in range(NCHUNK)], axis=0)
+                    zrow[c * CHUNK + i] = v.astype(jnp.bfloat16)
                     return 0
 
                 lax.fori_loop(0, CHUNK, turn_out, 0)
@@ -328,13 +373,8 @@
 
 
 def local_fn(pair_act, pair_mask, in_gamma, in_beta, w_proj, w_gate, out_gamma, out_beta, w_out):
-    mask = jnp.pad(pair_mask.astype(jnp.float32), ((0, 0), (0, 128 - BLK)))
-
-    def spread(v):
-        return jnp.broadcast_to(v.reshape(UPDATES, C, 1), (UPDATES, C, 128))
-
-    def turned(w):
-        return jnp.swapaxes(w.reshape((UPDATES,) + w.shape[2:]), 1, 2)
+    def flat(w):
+        return w.reshape((UPDATES,) + w.shape[2:])
 
     any_spec = pl.BlockSpec(memory_space=pl.ANY)
     vmem = pl.BlockSpec(memory_space=pltpu.VMEM)
@@ -342,9 +382,17 @@
     return pl.pallas_call(
         kernel,
         out_shape=jax.ShapeDtypeStruct((BLK, BLK, C), bf16),
-        in_specs=[any_spec, any_spec] + [vmem] * 7,
+        in_specs=[any_spec] + [vmem] * 8,
         out_specs=any_spec,
         scratch_shapes=[
+            pltpu.VMEM((UPDATES, 4 * C, C), bf16),
+            pltpu.VMEM((UPDATES, C, C), bf16),
+            pltpu.VMEM((UPDATES, C, C), bf16),
+            pltpu.VMEM((UPDATES, C, C), f32),
+            pltpu.VMEM((UPDATES, C, C), f32),
+            pltpu.VMEM((UPDATES, C, C), f32),
+            pltpu.VMEM((UPDATES, C, C), f32),
+            pltpu.VMEM((BLK, 128), f32),
             pltpu.VMEM((ROWS, N, C), bf16),
             pltpu.VMEM((4, ROWS, 128), f32),
             pltpu.VMEM((ROWS, N), f32),
@@ -375,8 +423,7 @@
         ],
         compiler_params=pltpu.CompilerParams(has_side_effects=True, vmem_limit_bytes=60 * 1024 * 1024),
         name="triangle",
-    )(pair_act, mask, spread(in_gamma), spread(in_beta), turned(w_proj), turned(w_gate),
-      spread(out_gamma), spread(out_beta), turned(w_out))
+    )(pair_act, pair_mask, in_gamma, in_beta, flat(w_proj), flat(w_gate), out_gamma, out_beta, flat(w_out))
 
 
 def solution(mesh):

time: 785 us -> 775 us (0.987)
  local copies, waits for them, and re-layouts: 14.8 us -> 3.22 us
where the time goes in v3:
time: 775 us; the launch traced here: 772 us
  Pallas kernels  769 us (99%)
    pallas_call x1, Pallas kernels, local_fn(): pl.pallas_call(kernel, out_shape=jax.ShapeDtypeStruct((BLK, BLK, C), bf16...  769 us

profile of v3, /device:TPU:10, one launch (start us, length us, event | category | flops | bytes accessed | tf_op | source)
XLA Modules:
  0.0 772.0 jit_solution(17168481951426055171)
XLA Ops:
  0.0 768.8 %triangle.1 = bf16[96,96,128]{2,1,0:T(8,128)(2,1)} custom-call(bf16[96,96,128]{2,1,0:T(8,128)(2,1)} %z_in.1, s32[96,96]{1,0:T(8,128)} %m_in.1, f32[4,2,128]{2,1,0:T(2,128)} %gin_in.1, f32[4,2,128]{2,1,0:T(2,128)} %bin_in.1, bf16[8,128,512]{2,1,0:T(8,128)(2,1)} %bitcast.3, bf16[8,128,128]{2,1,0:T(8,128)(2,1)} %bitcast.4, f32[4,2,128]{2,1,0:T(2,128)} %gout_in.1, ...), custom_call_target="tpu_custom_call" | custom-call | tf_op jit(solution)/shard_map/triangle/pallas_call | solution.py:382
  768.8 3.2 copy.11

commit v4 on v3

--- a/solution.py
+++ b/solution.py
@@ -19,6 +19,7 @@
 NCHUNK = ROWS // CHUNK
 LT = N // 128
 UPDATES = 8
+GROUP = 2 * LT
 
 
 def sigmoid(x):
@@ -155,61 +156,69 @@
     for j in range(4):
         pick = jnp.logical_and(natural == lane + j * BLK, lane < BLK).astype(jnp.float32)
         total = total + jnp.dot(mrow[j], pick, preferred_element_type=jnp.float32)
-    mask[...] = total
-
-    def project(u, p):
-        for h in range(2):
-            for lt in range(LT):
-                v = z[2 * p + h, :, pl.ds(lt * 128, 128)].astype(jnp.float32)
-                xn = norm_channels(v, gin[u], bin_[u])
-                x[:, pl.ds(h * N + lt * 128, 128)] = xn.astype(jnp.bfloat16)
+    for i in range(ROWS):
+        mask[i] = total[i:i + 1, :]
+
+    def pieces(by_row, c, p):
+        if by_row:
+            return [(c * CHUNK + 2 * p + h, lt) for h in range(2) for lt in range(LT)]
+        return [(p * GROUP + e, c) for e in range(GROUP)]
+
+    def lanes(lt, n=1):
+        return pl.ds(lt * 128, n * 128)
+
+    def project(u, group):
+        for e, (row, lt) in enumerate(group):
+            v = z[row, :, lanes(lt)].astype(jnp.float32)
+            x[:, lanes(e)] = norm_channels(v, gin[u], bin_[u]).astype(jnp.bfloat16)
         q[pl.ds(0, 4 * C), :] = jnp.dot(wp[u], x[...], preferred_element_type=jnp.float32)
         q[pl.ds(4 * C, C), :] = jnp.dot(wg[u], x[...], preferred_element_type=jnp.float32)
-        for h in range(2):
-            cols = pl.ds(h * N, N)
-            m = mask[pl.ds(2 * p + h, 1), :]
-            for d in range(D):
-                def part(k):
-                    return q[pl.ds(k * C + d * CPD, CPD), cols]
-                left = m * sigmoid(part(1)) * part(0)
-                right = m * sigmoid(part(3)) * part(2)
-                ab[d, 2 * p + h] = jnp.concatenate([left, right], axis=0).astype(jnp.bfloat16)
-                gate[2 * p + h, pl.ds(d * CPD, CPD), :] = sigmoid(part(4))
-
-    def finish(u, p):
-        for lt in range(LT):
-            tv = trecv[:, p, :, pl.ds(lt * 128, 128)].astype(jnp.float32)
-            for h in range(2):
-                v = tv[:, h * CPD:(h + 1) * CPD, :].reshape(C, 128)
-                yn = norm_channels(v, gout[u], bout[u])
-                y[:, pl.ds(h * N + lt * 128, 128)] = yn.astype(jnp.bfloat16)
+        for e, (row, lt) in enumerate(group):
+            m = mask[row, :, lanes(lt)]
+
+            def part(k):
+                return q[pl.ds(k * C, C), lanes(e)]
+            left = (m * sigmoid(part(1)) * part(0)).reshape(D, CPD, 128)
+            right = (m * sigmoid(part(3)) * part(2)).reshape(D, CPD, 128)
+            both = jnp.concatenate([left, right], axis=1).astype(jnp.bfloat16)
+            ab[:, row // CHUNK, row % CHUNK, :, lanes(lt)] = both
+            gate[row, :, lanes(lt)] = sigmoid(part(4))
+
+    def finish(u, by_row, group):
+        for e, (row, lt) in enumerate(group):
+            h = e // LT if by_row else e % 2
+            tv = trecv[:, row // 2, :, lanes(lt)].astype(jnp.float32)
+            v = tv[:, h * CPD:(h + 1) * CPD, :].reshape(C, 128)
+            y[:, lanes(e)] = norm_channels(v, gout[u], bout[u]).astype(jnp.bfloat16)
         q[pl.ds(0, C), :] = jnp.dot(wo[u], y[...], preferred_element_type=jnp.float32)
-        for h in range(2):
-            for k in range(C // 16):
-                rows = pl.ds(k * 16, 16)
-                upd = gate[2 * p + h, rows, :] * q[rows, pl.ds(h * N, N)]
-                z[2 * p + h, rows, :] = (z[2 * p + h, rows, :].astype(jnp.float32) + upd).astype(jnp.bfloat16)
-
-    def send_ab(c):
-        mine = pl.ds(pl.multiple_of(c * 128 + me * CHUNK, 8), CHUNK)
-        rows = pl.ds(c * CHUNK, CHUNK)
-
+        for e, (row, lt) in enumerate(group):
+            upd = gate[row, :, lanes(lt)] * q[pl.ds(0, C), lanes(e)]
+            z[row, :, lanes(lt)] = (z[row, :, lanes(lt)].astype(jnp.float32) + upd).astype(jnp.bfloat16)
+
+    def send_ab(by_row, c):
         def to(d, _):
             dst, num = place(d)
-            pltpu.make_async_remote_copy(ab.at[num, rows], r.at[mine], absend_sem, abrecv_sem.at[c],
-                                         device_id=dst, device_id_type=MESH).start()
+            if by_row:
+                src, into = ab.at[num, c], r.at[c, me]
+            else:
+                src, into = ab.at[num, :, :, :, lanes(c)], r.at[:, me, :, :, lanes(c)]
+            pltpu.make_async_remote_copy(src, into, absend_sem, abrecv_sem.at[c], device_id=dst, device_id_type=MESH).start()
             return 0
 
         lax.fori_loop(0, D - 1, to, 0)
-        r[mine] = ab[me, rows]
-
-    def project_chunk(u, c):
+        if by_row:
+            r[c, me] = ab[me, c]
+        else:
+            for e in range(NCHUNK):
+                r[e, me, :, :, lanes(c)] = ab[me, e, :, :, lanes(c)]
+
+    def project_chunk(u, by_row, c):
         def one(p, _):
-            project(u, c * (CHUNK // 2) + p)
-            return 0
-
-        lax.fori_loop(0, CHUNK // 2, one, 0)
-        send_ab(c)
+            project(u, pieces(by_row, c, p))
+            return 0
+
+        lax.fori_loop(0, ROWS * LT // NCHUNK // GROUP, one, 0)
+        send_ab(by_row, c)
 
     for c in range(NCHUNK):
         got = zrow.at[pl.ds(c * CHUNK, CHUNK)]
@@ -223,7 +232,7 @@
             return 0
 
         lax.fori_loop(0, CHUNK, turn_in, 0)
-        project_chunk(0, c)
+        project_chunk(0, True, c)
     for q_ in range(4):
         mask_out(q_, False)
         for c in range(NCHUNK):
@@ -251,102 +260,102 @@
             def _():
                 pltpu.make_async_copy(src, into, orecv_sem).start()
 
-    def update(u, _):
-        def block(ch, c, lts=range(LT)):
-            rows = pl.ds(c * 128, 128)
-            return jnp.concatenate([s[ch, lt, rows, :] for lt in lts], axis=1).astype(jnp.bfloat16)
-
-        def dot(lhs, rhs, dim):
-            return lax.dot_general(lhs, rhs, (((dim,), (dim,)), ((), ())), preferred_element_type=jnp.float32)
-
-        def outer(rows, lts):
-            def one(ch, _):
-                right = [block(ch + CPD, lt) for lt in lts]
-                right = jnp.concatenate(right, axis=0)
-                for i in rows:
-                    prod = dot(block(ch, i), right, 1)
-                    for n, lt in enumerate(lts):
-                        t[ch, lt, pl.ds(i * 128, 128), :] = prod[:, n * 128:(n + 1) * 128]
-                return 0
-
-            @pl.when(u % 2 == 0)
-            def _():
-                lax.fori_loop(0, CPD, one, 0)
-
-        def inner(rows, c):
-            def one(ch, _):
-                right = block(ch + CPD, c)
-                for i in rows:
-                    prod = dot(block(ch, c, (i,)), right, 0)
-                    for lt in range(LT):
-                        at = pl.ds(i * 128, 128)
-                        part = prod[:, lt * 128:(lt + 1) * 128]
-                        t[ch, lt, at, :] = part if c == 0 else t[ch, lt, at, :] + part
-                return 0
-
-            @pl.when(u % 2 == 1)
-            def _():
-                lax.fori_loop(0, CPD, one, 0)
-
+    def block(ch, i, outgoing):
+        if outgoing:
+            return jnp.concatenate([s[ch, lt, pl.ds(i * 128, 128), :] for lt in range(LT)], axis=1).astype(jnp.bfloat16)
+        return s[ch, i].astype(jnp.bfloat16)
+
+    def multiply(outgoing, rows, cols):
+        dims = ((1,), (1,)) if outgoing else ((0,), (0,))
+
+        def one(ch, _):
+            right = jnp.concatenate([block(ch + CPD, lt, outgoing) for lt in cols], axis=0 if outgoing else 1)
+            for i in rows:
+                prod = lax.dot_general(block(ch, i, outgoing), right, (dims, ((), ())), preferred_element_type=jnp.float32)
+                for n, lt in enumerate(cols):
+                    t[ch, lt, pl.ds(i * 128, 128), :] = prod[:, n * 128:(n + 1) * 128]
+            return 0
+
+        lax.fori_loop(0, CPD, one, 0)
+
+    def give(chunk, rows, cols):
+        def to(n, _):
+            dst, num = place(n)
+            for i in rows:
+                at = pl.ds(pl.multiple_of(i * 128 + num * CHUNK, 8), CHUNK)
+                for lt in cols:
+                    v = jnp.swapaxes(t[:, lt, at, :], 0, 1)
+                    tsend[num, pl.ds(i * (CHUNK // 2), CHUNK // 2), :, lanes(lt)] = (
+                        v.reshape(CHUNK // 2, 16, 128).astype(jnp.bfloat16))
+            pairs = pl.ds(rows[0] * (CHUNK // 2), len(rows) * (CHUNK // 2))
+            wide = lanes(cols[0], len(cols))
+
+            @pl.when(n < D - 1)
+            def _():
+                pltpu.make_async_remote_copy(tsend.at[num, pairs, :, wide], trecv.at[me, pairs, :, wide], tsend_sem,
+                                             trecv_sem.at[chunk], device_id=dst, device_id_type=MESH).start()
+
+            @pl.when(n == D - 1)
+            def _():
+                trecv[me, pairs, :, wide] = tsend[num, pairs, :, wide]
+            return 0
+
+        lax.fori_loop(0, D, to, 0)
+
+    def gather(by_row, c):
+        part = r.at[c, pl.ds(0, D - 1)]
+        pltpu.make_async_copy(part, part, abrecv_sem.at[c]).wait()
+
+        def turn(k, _):
+            for e in (c,) if by_row else range(NCHUNK):
+                rows = pl.ds(pl.multiple_of(e * 128 + k * CHUNK, 8), CHUNK)
+                for lt in range(LT) if by_row else (c,):
+                    v = r[e, k, :, :, lanes(lt)].astype(jnp.float32)
+                    s[:, lt, rows, :] = jnp.swapaxes(v, 0, 1)
+            return 0
+
+        lax.fori_loop(0, D, turn, 0)
+
+    def update(u, outgoing):
+        gather(outgoing, 0)
+        multiply(outgoing, (0,), (0,))
+        gather(outgoing, 1)
+        multiply(outgoing, (0,), (1,))
+        multiply(outgoing, (1,), (0, 1))
+        for c in range(2):
+            if outgoing:
+                give(c, (0, 1), (c,))
+            else:
+                give(c, (c,), (0, 1))
+        gather(outgoing, 2)
+        for c in range(2):
+            rows, cols = ((2,), (c,)) if outgoing else ((c,), (2,))
+            multiply(outgoing, rows, cols)
+            give(c, rows, cols)
+        rows, cols = (range(NCHUNK), (2,)) if outgoing else ((2,), range(NCHUNK))
+        multiply(outgoing, rows, cols)
+        give(2, rows, cols)
+
+        by_row = not outgoing
         for c in range(NCHUNK):
-            part = r.at[pl.ds(0, (D - 1) * CHUNK)]
-            pltpu.make_async_copy(part, part, abrecv_sem.at[c]).wait()
-
-            def turn(k, _):
-                rows = pl.ds(pl.multiple_of(c * 128 + k * CHUNK, 8), CHUNK)
-                for lt in range(LT):
-                    v = r[rows, :, pl.ds(lt * 128, 128)].astype(jnp.float32)
-                    s[:, lt, rows, :] = jnp.swapaxes(v, 0, 1)
-                return 0
-
-            lax.fori_loop(0, D, turn, 0)
-            if c < NCHUNK - 1:
-                outer(range(c), (c,))
-                outer((c,), range(c + 1))
-                inner(range(LT), c)
-
-        last = NCHUNK - 1
-        for c in range(NCHUNK):
-            outer((c,), range(NCHUNK) if c == last else (last,))
-            inner((c,), last)
-
-            def give(n, _):
-                dst, num = place(n)
-                rows = pl.ds(pl.multiple_of(c * 128 + num * CHUNK, 8), CHUNK)
-                pairs = pl.ds(num * (ROWS // 2) + c * (CHUNK // 2), CHUNK // 2)
-                into = pl.ds(c * (CHUNK // 2), CHUNK // 2)
-                for lt in range(LT):
-                    v = jnp.swapaxes(t[:, lt, rows, :], 0, 1)
-                    tsend[pairs, :, pl.ds(lt * 128, 128)] = v.reshape(CHUNK // 2, 16, 128).astype(jnp.bfloat16)
-
-                @pl.when(n < D - 1)
-                def _():
-                    pltpu.make_async_remote_copy(tsend.at[pairs], trecv.at[me, into], tsend_sem, trecv_sem.at[c],
-                                                 device_id=dst, device_id_type=MESH).start()
-
-                @pl.when(n == D - 1)
-                def _():
-                    trecv[me, into] = tsend[pairs]
-                return 0
-
-            lax.fori_loop(0, D, give, 0)
-
-        for c in range(NCHUNK):
-            part = tsend.at[pl.ds(0, (D - 1) * (CHUNK // 2))]
+            part = trecv.at[pl.ds(0, D - 1), pl.ds(0, CHUNK // 2)]
             pltpu.make_async_copy(part, part, trecv_sem.at[c]).wait()
             if c == 0:
                 part = ab.at[pl.ds(0, D - 1)]
                 pltpu.make_async_copy(part, part, absend_sem).wait()
 
             def one(p, _):
-                finish(u, c * (CHUNK // 2) + p)
+                finish(u, by_row, pieces(by_row, c, p))
                 return 0
 
-            lax.fori_loop(0, CHUNK // 2, one, 0)
+            lax.fori_loop(0, ROWS * LT // NCHUNK // GROUP, one, 0)
+            if outgoing:
+                project_chunk(u + 1, by_row, c)
+                continue
 
             @pl.when(u < UPDATES - 1)
             def _():
-                project_chunk(jnp.minimum(u + 1, UPDATES - 1), c)
+                project_chunk(jnp.minimum(u + 1, UPDATES - 1), by_row, c)
 
             @pl.when(u == UPDATES - 1)
             def _():
@@ -360,11 +369,15 @@
                 lax.fori_loop(0, CHUNK, turn_out, 0)
                 for j in range(4):
                     block_back(j, c, True)
-        part = tsend.at[pl.ds(0, (D - 1) * (ROWS // 2))]
+        part = tsend.at[pl.ds(0, D - 1)]
         pltpu.make_async_copy(part, part, tsend_sem).wait()
+
+    def both(n, _):
+        update(2 * n, True)
+        update(2 * n + 1, False)
         return 0
 
-    lax.fori_loop(0, UPDATES, update, 0)
+    lax.fori_loop(0, UPDATES // 2, both, 0)
 
     pltpu.make_async_copy(out, out, orecv_sem).wait()
     for c in range(NCHUNK):
@@ -395,17 +408,17 @@
             pltpu.VMEM((BLK, 128), f32),
             pltpu.VMEM((ROWS, N, C), bf16),
             pltpu.VMEM((4, ROWS, 128), f32),
-            pltpu.VMEM((ROWS, N), f32),
+            pltpu.VMEM((ROWS, 1, N), f32),
             pltpu.VMEM((ROWS, C, N), bf16),
             pltpu.VMEM((ROWS, C, N), f32),
             pltpu.VMEM((C, 2 * N), bf16),
             pltpu.VMEM((5 * C, 2 * N), f32),
             pltpu.VMEM((C, 2 * N), bf16),
-            pltpu.VMEM((D, ROWS, 2 * CPD, N), bf16),
-            pltpu.VMEM((N, 2 * CPD, N), bf16),
+            pltpu.VMEM((D, NCHUNK, CHUNK, 2 * CPD, N), bf16),
+            pltpu.VMEM((NCHUNK, D, CHUNK, 2 * CPD, N), bf16),
             pltpu.VMEM((2 * CPD, LT, N, 128), f32),
             pltpu.VMEM((CPD, LT, N, 128), f32),
-            pltpu.VMEM((N // 2, 2 * CPD, N), bf16),
+            pltpu.VMEM((D, ROWS // 2, 2 * CPD, N), bf16),
             pltpu.VMEM((D, ROWS // 2, 2 * CPD, N), bf16),
             pltpu.VMEM((2, ROWS, BLK, C), bf16),
             pltpu.SemaphoreType.DMA((4, NCHUNK)),

time: 775 us -> 743 us (0.959)
  Pallas kernels: 769 us -> 738 us
    pallas_call x1, Pallas kernels: 769 us -> 738 us  [local_fn(): pl.pallas_call(kernel, out_shape=jax.ShapeDtypeStruct((BLK, BLK, C), bf16...]
where the time goes in v4:
time: 743 us; the launch traced here: 741 us
  Pallas kernels  738 us (99%)
    pallas_call x1, Pallas kernels, local_fn(): pl.pallas_call(kernel, out_shape=jax.ShapeDtypeStruct((BLK, BLK, C), bf16...  738 us

profile of v4, /device:TPU:10, one launch (start us, length us, event | category | flops | bytes accessed | tf_op | source)
XLA Modules:
  0.0 741.2 jit_solution(3616626322892521401)
XLA Ops:
  0.0 738.0 %triangle.1 = bf16[96,96,128]{2,1,0:T(8,128)(2,1)} custom-call(bf16[96,96,128]{2,1,0:T(8,128)(2,1)} %z_in.1, s32[96,96]{1,0:T(8,128)} %m_in.1, f32[4,2,128]{2,1,0:T(2,128)} %gin_in.1, f32[4,2,128]{2,1,0:T(2,128)} %bin_in.1, bf16[8,128,512]{2,1,0:T(8,128)(2,1)} %bitcast.3, bf16[8,128,128]{2,1,0:T(8,128)(2,1)} %bitcast.4, f32[4,2,128]{2,1,0:T(2,128)} %gout_in.1, ...), custom_call_target="tpu_custom_call" | custom-call | tf_op jit(solution)/shard_map/triangle/pallas_call | solution.py:395
  738.0 3.2 copy.11

commit v5 on v4

--- a/solution.py
+++ b/solution.py
@@ -17,6 +17,8 @@
 CPD = C // D
 CHUNK = 8
 NCHUNK = ROWS // CHUNK
+FEW = 4
+NFEW = ROWS // FEW
 LT = N // 128
 UPDATES = 8
 GROUP = 2 * LT
@@ -63,8 +65,9 @@
 
     def block_out(q_, c, start):
         px, pz = q_ // 2, 2 * g + q_ % 2
-        rows = pl.ds(c * CHUNK, CHUNK)
-        src = z_in.at[pl.ds(q_ * ROWS + c * CHUNK, CHUNK)]
+        rows = pl.ds(c * FEW, FEW)
+        src = z_in.at[pl.ds(q_ * ROWS + c * FEW, FEW)]
+        done = zrecv_sem.at[c * FEW // CHUNK]
         into = zrow.at[rows, cols(jz), :]
         stay = px == g
         there = pz == jz
@@ -77,7 +80,7 @@
 
         @pl.when(jnp.logical_or(jnp.logical_and(stay, jnp.logical_not(there)), jnp.logical_and(jnp.logical_not(stay), there)))
         def _():
-            go(pltpu.make_async_remote_copy(src, into, zsend_sem.at[q_, c], zrecv_sem.at[c],
+            go(pltpu.make_async_remote_copy(src, into, zsend_sem.at[q_, c], done,
                                             device_id=(px, pz, iy), device_id_type=MESH))
 
         @pl.when(jnp.logical_and(jnp.logical_not(stay), jnp.logical_not(there)))
@@ -88,16 +91,17 @@
         if start:
             @pl.when(jnp.logical_and(stay, there))
             def _():
-                pltpu.make_async_copy(src, into, zrecv_sem.at[c]).start()
+                pltpu.make_async_copy(src, into, done).start()
 
     def pass_on(zq, c, start):
-        rows = pl.ds(c * CHUNK, CHUNK)
+        rows = pl.ds(c * FEW, FEW)
         pz = 2 * (1 - g) + zq
 
         @pl.when(pz != jz)
         def _():
             copy = pltpu.make_async_remote_copy(relay.at[zq, rows], zrow.at[rows, cols(jz), :], fsend_sem.at[zq, c],
-                                                zrecv_sem.at[c], device_id=(g, pz, iy), device_id_type=MESH)
+                                                zrecv_sem.at[c * FEW // CHUNK], device_id=(g, pz, iy),
+                                                device_id_type=MESH)
             if start:
                 got = relay.at[zq, rows]
                 pltpu.make_async_copy(got, got, lrecv_sem.at[zq, c]).wait()
@@ -124,7 +128,7 @@
             def _():
                 mrow[jz] = msend[rows]
 
-    for c in range(NCHUNK):
+    for c in range(NFEW):
         for q_ in range(4):
             block_out(q_, c, True)
     msend[...] = jnp.zeros_like(msend)
@@ -140,8 +144,9 @@
             dst[u] = jnp.broadcast_to(src[u // 2, pl.ds(u % 2, 1), :], (C, C)).T
         return 0
 
-    lax.fori_loop(0, UPDATES, prepare, 0)
-    for c in range(NCHUNK):
+    for c in range(NFEW):
+        if c > 0:
+            lax.fori_loop(2 * c - 2, min(2 * c, UPDATES), prepare, 0)
         for zq in range(2):
             pass_on(zq, c, True)
     for n_from in (3, 4):
@@ -196,16 +201,21 @@
             z[row, :, lanes(lt)] = (z[row, :, lanes(lt)].astype(jnp.float32) + upd).astype(jnp.bfloat16)
 
     def send_ab(by_row, c):
-        def to(d, _):
-            dst, num = place(d)
+        parts = 4 if by_row else 3
+
+        def to(n, _):
+            dst, num = place(n % (D - 1))
+            e = n // (D - 1)
             if by_row:
-                src, into = ab.at[num, c], r.at[c, me]
-            else:
-                src, into = ab.at[num, :, :, :, lanes(c)], r.at[:, me, :, :, lanes(c)]
+                some = pl.ds(e * (CHUNK // parts), CHUNK // parts)
+                src, into = ab.at[num, c, some], r.at[c, me, some]
+            else:
+                some = pl.ds(e * (NCHUNK // parts), NCHUNK // parts)
+                src, into = ab.at[num, some, :, :, lanes(c)], r.at[some, me, :, :, lanes(c)]
             pltpu.make_async_remote_copy(src, into, absend_sem, abrecv_sem.at[c], device_id=dst, device_id_type=MESH).start()
             return 0
 
-        lax.fori_loop(0, D - 1, to, 0)
+        lax.fori_loop(0, parts * (D - 1), to, 0)
         if by_row:
             r[c, me] = ab[me, c]
         else:
@@ -235,9 +245,9 @@
         project_chunk(0, True, c)
     for q_ in range(4):
         mask_out(q_, False)
-        for c in range(NCHUNK):
+        for c in range(NFEW):
             block_out(q_, c, False)
-    for c in range(NCHUNK):
+    for c in range(NFEW):
         for zq in range(2):
             pass_on(zq, c, False)
 
@@ -421,12 +431,12 @@
             pltpu.VMEM((D, ROWS // 2, 2 * CPD, N), bf16),
             pltpu.VMEM((D, ROWS // 2, 2 * CPD, N), bf16),
             pltpu.VMEM((2, ROWS, BLK, C), bf16),
-            pltpu.SemaphoreType.DMA((4, NCHUNK)),
+            pltpu.SemaphoreType.DMA((4, NFEW)),
             pltpu.SemaphoreType.DMA((4,)),
-            pltpu.SemaphoreType.DMA((2, NCHUNK)),
+            pltpu.SemaphoreType.DMA((2, NFEW)),
             pltpu.SemaphoreType.DMA((NCHUNK,)),
             pltpu.SemaphoreType.DMA,
-            pltpu.SemaphoreType.DMA((2, NCHUNK)),
+            pltpu.SemaphoreType.DMA((2, NFEW)),
             pltpu.SemaphoreType.DMA,
             pltpu.SemaphoreType.DMA((NCHUNK,)),
             pltpu.SemaphoreType.DMA,

time: 743 us -> 739 us (level)
  no operation moved by 1% of the time
where the time goes in v5:
time: 739 us; the launch traced here: 737 us
  Pallas kernels  734 us (99%)
    pallas_call x1, Pallas kernels, local_fn(): pl.pallas_call(kernel, out_shape=jax.ShapeDtypeStruct((BLK, BLK, C), bf16...  734 us

profile of v5, /device:TPU:10, one launch (start us, length us, event | category | flops | bytes accessed | tf_op | source)
XLA Modules:
  0.0 736.9 jit_solution(563964681013970510)
XLA Ops:
  0.0 733.7 %triangle.1 = bf16[96,96,128]{2,1,0:T(8,128)(2,1)} custom-call(bf16[96,96,128]{2,1,0:T(8,128)(2,1)} %z_in.1, s32[96,96]{1,0:T(8,128)} %m_in.1, f32[4,2,128]{2,1,0:T(2,128)} %gin_in.1, f32[4,2,128]{2,1,0:T(2,128)} %bin_in.1, bf16[8,128,512]{2,1,0:T(8,128)(2,1)} %bitcast.3, bf16[8,128,128]{2,1,0:T(8,128)(2,1)} %bitcast.4, f32[4,2,128]{2,1,0:T(2,128)} %gout_in.1, ...), custom_call_target="tpu_custom_call" | custom-call | tf_op jit(solution)/shard_map/triangle/pallas_call | solution.py:405
  733.7 3.2 copy.11
